TPU v7x, 8 devices: a whole 2x2x1 slice. The times are simulated.
8 devices in a mesh: kpt: 1 (over z), col: 2 (over y), row: 4 (over x, core).
Axes of the slice: x: 2, y: 2, z: 1, core: 2. Of those that a mesh axis runs over, the one named last changes fastest.
Arguments:
- z_in: float32 [6144, 1024], P('kpt', ('col', 'row'))
- v_panels: float32 [6144, 6144], P(('kpt', 'row'), 'col')
- t_factors: float32 [192, 32, 32], P('kpt')
Outputs:
- output: float32 [6144, 1024], P(('kpt', 'row'), 'col')
All inputs are finite; a program needn't handle non-finite values.
Results may differ from a plain program's by a relative error of at most 0.001.
Values sent between devices are 32-bit elements.
A program may use at most 1 GiB of HBM per device.

v0:
```python
import jax
import jax.numpy as jnp
from jax import lax
from jax.sharding import PartitionSpec as P

PRECISE = lax.Precision.HIGHEST


def solution(mesh):
    col_count = mesh.shape["col"]

    def local_run(z_cols, v_local, t_local):
        panel_width = t_local.shape[-1]
        group_count = v_local.shape[1] // panel_width
        z_cur = lax.all_to_all(z_cols, "row", 0, 1, tiled=True)

        def group_step(step_idx, z_acc):
            group_idx = group_count - 1 - step_idx
            own_panel = lax.dynamic_slice_in_dim(v_local, group_idx * panel_width, panel_width, axis=1)
            gathered = lax.all_gather(own_panel, "col")

            def panel_step(inner_idx, z_val):
                owner_col = col_count - 1 - inner_idx
                panel = lax.dynamic_index_in_dim(gathered, owner_col, axis=0, keepdims=False)
                t_mat = lax.dynamic_index_in_dim(t_local, group_idx * col_count + owner_col, axis=0, keepdims=False)
                s_part = jnp.einsum("lb,lm->bm", panel, z_val, precision=PRECISE, preferred_element_type=jnp.float32)
                s_full = lax.psum(s_part, "row")
                w_full = jnp.dot(t_mat, s_full, precision=PRECISE, preferred_element_type=jnp.float32)
                return z_val - jnp.dot(panel, w_full, precision=PRECISE, preferred_element_type=jnp.float32)

            return lax.fori_loop(0, col_count, panel_step, z_acc)

        return lax.fori_loop(0, group_count, group_step, z_cur)

    return jax.shard_map(
        local_run,
        mesh=mesh,
        in_specs=(P("kpt", ("col", "row")), P(("kpt", "row"), "col"), P("kpt", None, None)),
        out_specs=P(("kpt", "row"), "col"),
        check_vma=False,
    )
```

profile of v0, /device:TPU:0, one launch (start us, length us, event | category | flops | bytes accessed | tf_op | source)
XLA Modules:
  0.0 8776.2 jit_solution(14828643695846529194)
XLA Ops:
  52.7 8715.0 %while.44 = (s32[]{:T(128)}, f32[1536,512]{1,0:T(8,128)S(1)}, f32[1536,3072]{1,0:T(8,128)}, f32[192,32,32]{2,1,0:T(8,128)}, s32[]{:T(128)}, /*index=5*/s32[]{:T(...) while((s32[]{:T(128)}, f32[1536,512]{1,0:T(8,128)S(1)}, ...), condition=%wide.region_4.5_spmd, body=%wide.region_0.4_spmd.sunk | while | flops 611074048 | bytes 12665356 | solution.py:33
  346.5 70.7 while.45
  437.3 70.7 while.45
  618.8 70.7 while.45
  709.6 70.7 while.45
  891.1 70.7 while.45
  981.9 70.7 while.45
  1163.4 70.7 while.45
  1254.2 70.7 while.45
  1435.7 70.7 while.45
  1526.5 70.7 while.45
  1708.0 70.7 while.45
  1798.8 70.7 while.45
  1980.3 70.7 while.45
  2071.1 70.7 while.45
  2252.6 70.7 while.45
  2343.4 70.7 while.45
  2524.9 70.7 while.45
  2615.7 70.7 while.45
  2797.2 70.7 while.45
  2888.0 70.7 while.45
  3069.5 70.7 while.45
  3160.3 70.7 while.45
  3341.8 70.7 while.45
  3432.6 70.7 while.45
  3614.1 70.7 while.45
  3704.8 70.7 while.45
  3886.4 70.7 while.45
  3977.1 70.7 while.45
  4158.7 70.7 while.45
  4249.4 70.7 while.45
  4521.7 70.7 while.45
  4794.0 70.7 while.45
  5066.3 70.7 while.45
  5338.6 70.7 while.45
  5610.9 70.7 while.45
  5883.2 70.7 while.45
  6064.7 70.7 while.45
  6155.5 70.7 while.45
  6427.8 70.7 while.45
  6700.1 70.7 while.45
  6972.4 70.7 while.45
  7244.7 70.7 while.45
  7517.0 70.7 while.45
  7789.3 70.7 while.45
  8061.6 70.7 while.45
  8333.9 70.7 while.45
  8606.2 70.7 while.45
  (1400 shorter events, 12215.1 us)
Async XLA Ops:
  6.5 41.4 all-to-all-start
  346.5 30.2 all-reduce.2.cloned.1.call-start
  437.3 30.2 all-reduce.2.cloned.1.call-start
  618.8 30.2 all-reduce.2.cloned.1.call-start
  709.6 30.2 all-reduce.2.cloned.1.call-start
  891.1 30.2 all-reduce.2.cloned.1.call-start
  981.9 30.2 all-reduce.2.cloned.1.call-start
  1163.4 30.2 all-reduce.2.cloned.1.call-start
  1254.2 30.2 all-reduce.2.cloned.1.call-start
  1435.7 30.2 all-reduce.2.cloned.1.call-start
  1526.5 30.2 all-reduce.2.cloned.1.call-start
  1708.0 30.2 all-reduce.2.cloned.1.call-start
  1798.8 30.2 all-reduce.2.cloned.1.call-start
  1980.3 30.2 all-reduce.2.cloned.1.call-start
  2071.1 30.2 all-reduce.2.cloned.1.call-start
  2252.6 30.2 all-reduce.2.cloned.1.call-start
  2343.4 30.2 all-reduce.2.cloned.1.call-start
  2524.9 30.2 all-reduce.2.cloned.1.call-start
  2615.7 30.2 all-reduce.2.cloned.1.call-start
  2797.2 30.2 all-reduce.2.cloned.1.call-start
  2888.0 30.2 all-reduce.2.cloned.1.call-start
  3069.5 30.2 all-reduce.2.cloned.1.call-start
  3160.3 30.2 all-reduce.2.cloned.1.call-start
  3341.8 30.2 all-reduce.2.cloned.1.call-start
  3432.6 30.2 all-reduce.2.cloned.1.call-start
  3614.1 30.2 all-reduce.2.cloned.1.call-start
  3704.8 30.2 all-reduce.2.cloned.1.call-start
  3886.4 30.2 all-reduce.2.cloned.1.call-start
  3977.1 30.2 all-reduce.2.cloned.1.call-start
  4158.7 30.2 all-reduce.2.cloned.1.call-start
  4249.4 30.2 all-reduce.2.cloned.1.call-start
  4431.0 30.2 all-reduce.2.cloned.1.call-start
  4521.7 30.2 all-reduce.2.cloned.1.call-start
  4794.0 30.2 all-reduce.2.cloned.1.call-start
  5066.3 30.2 all-reduce.2.cloned.1.call-start
  5338.6 30.2 all-reduce.2.cloned.1.call-start
  5610.9 30.2 all-reduce.2.cloned.1.call-start
  5883.2 30.2 all-reduce.2.cloned.1.call-start
  6155.5 30.2 all-reduce.2.cloned.1.call-start
  6427.8 30.2 all-reduce.2.cloned.1.call-start
  6700.1 30.2 all-reduce.2.cloned.1.call-start
  6972.4 30.2 all-reduce.2.cloned.1.call-start
  7244.7 30.2 all-reduce.2.cloned.1.call-start
  7517.0 30.2 all-reduce.2.cloned.1.call-start
  7789.3 30.2 all-reduce.2.cloned.1.call-start
  8061.6 30.2 all-reduce.2.cloned.1.call-start
  8333.9 30.2 all-reduce.2.cloned.1.call-start
  8606.2 30.2 all-reduce.2.cloned.1.call-start
  (146 other events, 4339.1 us)
Sparse Core Ops, SparseCore 0:
  350.3 26.4 all-reduce.1
  441.1 26.4 all-reduce.1
  622.6 26.4 all-reduce.1
  713.3 26.4 all-reduce.1
  894.9 26.4 all-reduce.1
  985.6 26.4 all-reduce.1
  1167.2 26.4 all-reduce.1
  1257.9 26.4 all-reduce.1
  1439.5 26.4 all-reduce.1
  1530.2 26.4 all-reduce.1
  1711.8 26.4 all-reduce.1
  1802.5 26.4 all-reduce.1
  1984.1 26.4 all-reduce.1
  2074.8 26.4 all-reduce.1
  2256.4 26.4 all-reduce.1
  2347.1 26.4 all-reduce.1
  2528.6 26.4 all-reduce.1
  2619.4 26.4 all-reduce.1
  2800.9 26.4 all-reduce.1
  2891.7 26.4 all-reduce.1
  3073.2 26.4 all-reduce.1
  3164.0 26.4 all-reduce.1
  3345.5 26.4 all-reduce.1
  3436.3 26.4 all-reduce.1
  3617.8 26.4 all-reduce.1
  3708.6 26.4 all-reduce.1
  3890.1 26.4 all-reduce.1
  3980.9 26.4 all-reduce.1
  4162.4 26.4 all-reduce.1
  4253.2 26.4 all-reduce.1
  4434.7 26.4 all-reduce.1
  4525.5 26.4 all-reduce.1
  4707.0 26.4 all-reduce.1
  4797.8 26.4 all-reduce.1
  5070.1 26.4 all-reduce.1
  5342.4 26.4 all-reduce.1
  5614.7 26.4 all-reduce.1
  5886.9 26.4 all-reduce.1
  6159.2 26.4 all-reduce.1
  6431.5 26.4 all-reduce.1
  6703.8 26.4 all-reduce.1
  6976.1 26.4 all-reduce.1
  7248.4 26.4 all-reduce.1
  7520.7 26.4 all-reduce.1
  7793.0 26.4 all-reduce.1
  8065.3 26.4 all-reduce.1
  8337.6 26.4 all-reduce.1
  8609.9 26.4 all-reduce.1
  (144 shorter events, 3748.8 us)
where the time goes:
time: 8810 us; the launch traced here: 8780 us
  waiting for transfers between devices  5090 us (58%)
  blocking collectives  1790 us (20%)
  matrix products  1720 us (20%)
  local copies, waits for them, and re-layouts  145 us (2%)
    psum x192, waiting for transfers between devices, panel_step(): s_full = lax.psum(s_part, 'row')  5060 us
    all_gather x96, blocking collectives, group_step(): gathered = lax.all_gather(own_panel, 'col')  1790 us
    dot_general x192, matrix products, panel_step(): jnp.dot(panel, w_full, precision=PRECISE, preferred_element_type=jnp.floa...  825 us
    dot_general x192, matrix products, panel_step(): jnp.einsum('lb,lm->bm', panel, z_val, precision=PRECISE, preferred_elemen...  690 us
    dot_general x192, matrix products, panel_step(): jnp.dot(t_mat, s_full, precision=PRECISE, preferred_element_type=jnp.floa...  201 us
  transfers between devices with their start and end apart: 193, of which 193 were waited for; matrix products, arithmetic and copies ran while one was open for 0% of the time, Pallas kernels for 0%

commit v1 on v0

v1 whole, which is shorter than its diff:
```python
import jax
import jax.numpy as jnp
from jax import lax
from jax.experimental import pallas as pl
from jax.experimental.pallas import tpu as pltpu
from jax.sharding import PartitionSpec as P

PRECISE = lax.Precision.HIGHEST
MESH = pl.DeviceIdType.MESH

W = 32
ROWS = 1536
TILE = 256
HALF = 128
NT = ROWS // TILE
NB = 24
VT = 4 * sum(range(1, NT + 1))
AHEAD = 12


def _dot(a, b, ca, cb):
    return lax.dot_general(a, b, (((ca,), (cb,)), ((), ())), precision=PRECISE, preferred_element_type=jnp.float32)


def _base(b):
    q, i = b // 4, b % 4
    return 4 * (NT * q - (q * (q - 1)) // 2) + i * (NT - q)


def _panel(idx):
    return jnp.where(idx < HALF, 2 * (idx // W), 2 * ((idx - HALF) // W) + 1)


def _kernel(zt_in, v_in, t0_in, out, vbuf, zt, t0, acc, srecv, wbuf, usend, urecv, ufull, tbuf,
            loc_sem, ys_sem, yr_sem, os_sem, or_sem, fs_sem, fr_sem, zs_sem, zr_sem,
            ss_sem, sr_sem, us_sem, ur_sem, hs_sem, hr_sem, misc_sem, outs_sem, outr_sem):
    ridx = lax.axis_index("row")
    y = lax.axis_index("col")
    x, c = ridx // 2, ridx % 2
    xn = {"row": (ridx + 2) % 4}
    sib = {"row": ridx + 1 - 2 * c}
    yn = {"col": 1 - y}

    barrier = pltpu.get_barrier_semaphore()
    for dev in (xn, sib, yn):
        pl.semaphore_signal(barrier, inc=1, device_id=dev, device_id_type=MESH)

    def remote(src, dst, send, recv, dev):
        return pltpu.make_async_remote_copy(src, dst, send, recv, device_id=dev, device_id_type=MESH)

    def slab(b, rho, par):
        start = (rho * VT + _base(b)) * TILE + 64 * (b % 4)
        return vbuf.at[pl.ds(pl.multiple_of(start, 64), ROWS - 64 * b), pl.ds(pl.multiple_of(par * HALF, HALF), HALF)]

    def v_local(b):
        return pltpu.make_async_copy(v_in.at[pl.ds(64 * b, ROWS - 64 * b), pl.ds(HALF * b, HALF)], slab(b, c, y), loc_sem.at[b])

    def v_y(b, par):
        return remote(slab(b, c, par), slab(b, c, par), ys_sem.at[b], yr_sem.at[b], yn)

    def v_own(b, rho):
        return remote(slab(b, rho, y), slab(b, rho, y), os_sem.at[b], or_sem.at[b], sib)

    def v_fwd(b, rho):
        return remote(slab(b, rho, 1 - y), slab(b, rho, 1 - y), fs_sem.at[b], fr_sem.at[b], sib)

    def v_issue(b):
        v_local(b).wait()
        v_y(b, y).start()
        v_own(b, c).start()

    def static_block(b, fn):
        for qq in range(NT):

            @pl.when(b // 4 == qq)
            def _(qq=qq):
                for ii in range(4):

                    @pl.when(b % 4 == ii)
                    def _(ii=ii):
                        fn(4 * qq + ii)

    def z_own(rho):
        return pltpu.make_async_copy(
            zt_in.at[:, pl.ds(pl.multiple_of((2 * x + rho) * ROWS, HALF), ROWS)],
            zt.at[x, :, pl.ds(rho * ROWS, ROWS)], misc_sem.at[rho])

    def z_chunk(t, j, g):
        off = (j // 2) * ROWS + t * TILE + (j % 2) * HALF
        return remote(
            zt_in.at[:, pl.ds(pl.multiple_of(2 * (1 - x) * ROWS + off, HALF), HALF)],
            zt.at[g, :, pl.ds(pl.multiple_of(off, HALF), HALF)],
            zs_sem.at[4 * t + j], zr_sem.at[4 * t + j], xn)

    t0_copy = pltpu.make_async_copy(t0_in, t0, misc_sem.at[2])

    for b in range(NB - 1, NB - 5, -1):
        v_local(b).start()
    for rho in range(2):
        z_own(rho).start()
    t0_copy.start()
    for b in range(NB - 5, -1, -1):
        v_local(b).start()
    for b in range(NB):
        if b % 4:
            for rho in range(2):
                vbuf[pl.ds((rho * VT + _base(b)) * TILE, 64 * (b % 4)), :] = jnp.zeros((64 * (b % 4), TILE), jnp.float32)

    pl.semaphore_wait(barrier, 3)
    for b in range(NB - 1, NB - 1 - AHEAD, -1):
        v_issue(b)
        if b == NB - 2:
            for j in range(4):
                z_chunk(NT - 1, j, x).start()
    for rho in range(2):
        z_own(rho).wait()
    t0_copy.wait()

    def rows(b, t, rho):
        return pl.ds(pl.multiple_of((rho * VT + _base(b) + t - b // 4) * TILE, TILE), TILE)

    def cols(t, rho):
        return pl.ds(pl.multiple_of(rho * ROWS + t * TILE, TILE), TILE)

    def s_copy(g, b):
        return remote(acc.at[g], srecv.at[g, b % 2], ss_sem.at[g], sr_sem.at[g, b % 2], xn)

    def weights(g, b):
        s_copy(g, b).wait_recv()
        s_sum = acc[g] + srecv[g, b % 2]
        wbuf[...] = _dot(s_sum, tbuf[b % 2], 1, 1)
        s_copy(g, b).wait_send()

    def update(g, b, t, rho):
        z_new = zt[g, :, cols(t, rho)] - _dot(wbuf[...], vbuf[rows(b, t, rho), :], 1, 1)
        zt[g, :, cols(t, rho)] = z_new
        return z_new

    def sweep(g, k):
        @pl.when(k < NB - 1)
        def _():
            weights(g, k + 1)

        acc[g] = jnp.zeros((HALF, TILE), jnp.float32)

        @pl.when(k % 4 == 3)
        def _():
            acc[g] += sum(_dot(zt[g, :, cols(k // 4, rho)], vbuf[rows(k, k // 4, rho), :], 1, 0) for rho in range(2))

        def tile(t, carry):
            acc[g] += sum(_dot(update(g, k + 1, t, rho), vbuf[rows(k, t, rho), :], 1, 0) for rho in range(2))
            return carry

        lax.fori_loop((k + 1) // 4, NT, tile, 0)
        s_copy(g, k).start()

    def u_copy(b):
        return remote(usend, urecv.at[b % 4], us_sem, ur_sem.at[b % 4], xn)

    def half_copy(b, half):
        part = ufull.at[b % 2, pl.ds(pl.multiple_of(half * HALF, HALF), HALF), :]
        return remote(part, part, hs_sem, hr_sem.at[b % 2], sib)

    def gram(b):
        def tile(t, total):
            for rho in range(2):
                v_own_cols = vbuf[rows(b, t, rho), pl.ds(pl.multiple_of(c * HALF, HALF), HALF)]
                usend[...] += _dot(v_own_cols, vbuf[rows(b, t, rho), :], 0, 0)
            return total

        usend[...] = jnp.zeros((HALF, TILE), jnp.float32)
        lax.fori_loop(b // 4, NT, tile, 0)
        u_copy(b).start()

    def u_half(b):
        u_copy(b).wait()
        total = usend[...] + urecv[b % 4]
        pa = 2 * (lax.broadcasted_iota(jnp.int32, (HALF, TILE), 0) // W) + c
        pb = _panel(lax.broadcasted_iota(jnp.int32, (HALF, TILE), 1))

        @pl.when(b < NB - 1)
        def _():
            half_copy(b + 1, c).wait_send()

        ufull[b % 2, pl.ds(pl.multiple_of(c * HALF, HALF), HALF), :] = jnp.where(pa < pb, total, 0.0)
        half_copy(b, c).start()

    def merge(b):
        half_copy(b, 1 - c).wait_recv()
        u_all = ufull[b % 2]
        even, odd = t0[b, 0], t0[b, 1]
        ra = lax.broadcasted_iota(jnp.int32, (HALF, HALF), 0) // W
        rb = lax.broadcasted_iota(jnp.int32, (HALF, HALF), 1) // W
        pairs = jnp.where(ra == rb, u_all[:HALF, HALF:], 0.0)
        slot = b % 2
        tbuf[slot, :HALF, :HALF] = even
        tbuf[slot, :HALF, HALF:] = -_dot(_dot(even, pairs, 1, 0), odd, 1, 0)
        tbuf[slot, HALF:, :HALF] = jnp.zeros((HALF, HALF), jnp.float32)
        tbuf[slot, HALF:, HALF:] = odd
        pa = _panel(lax.broadcasted_iota(jnp.int32, (TILE, TILE), 0))
        pb = _panel(lax.broadcasted_iota(jnp.int32, (TILE, TILE), 1))
        for size in (2, 4):
            level = (pa // (2 * size) == pb // (2 * size)) & (pa // size < pb // size)
            t_now = tbuf[slot]
            tbuf[slot] = t_now - _dot(t_now, _dot(jnp.where(level, u_all, 0.0), t_now, 1, 0), 1, 0)

    def step(s, carry):
        k = NB + 2 - s

        @pl.when(k < NB)
        def _():
            @pl.when(k % 4 == 3)
            def _():
                for j in range(4):
                    z_chunk(k // 4, j, 1 - x).wait_recv()

            sweep(0, k)
            sweep(1, k)

            @pl.when(k >= 4)
            def _():
                z_chunk(k // 4 - 1, 3 - k % 4, x).start()

            @pl.when(k >= AHEAD)
            def _():
                static_block(k - AHEAD, v_issue)

        @pl.when((k >= 1) & (k <= NB))
        def _():
            u_half(k - 1)

        @pl.when(k >= 3)
        def _():
            def forward(b):
                v_y(b, 1 - y).wait_recv()
                v_fwd(b, c).start()

            static_block(k - 3, forward)

        @pl.when((k >= 2) & (k < NB + 2))
        def _():
            def arrived(b):
                v_own(b, 1 - c).wait_recv()
                v_fwd(b, 1 - c).wait_recv()

            static_block(k - 2, arrived)
            gram(k - 2)

        @pl.when((k >= 1) & (k <= NB))
        def _():
            merge(k - 1)

        return carry

    lax.fori_loop(0, NB + 3, step, 0)

    def out_rows(g):
        return pl.ds(pl.multiple_of((2 * g + c) * HALF, HALF), HALF)

    def out_local(g):
        return pltpu.make_async_copy(zt.at[g, :, pl.ds(pl.multiple_of(c * ROWS, HALF), ROWS)], out.at[out_rows(g), :], misc_sem.at[g])

    def out_sib(g):
        return remote(zt.at[g, :, pl.ds(pl.multiple_of((1 - c) * ROWS, HALF), ROWS)], out.at[out_rows(g), :],
                      outs_sem.at[g], outr_sem.at[g], sib)

    def out_from_sib(g):
        part = out.at[pl.ds(pl.multiple_of((2 * g + 1 - c) * HALF, HALF), HALF), :]
        return remote(part, part, outs_sem.at[g], outr_sem.at[g], sib)

    for g in range(2):
        weights(g, 0)

        def last(t, carry, g=g):
            for rho in range(2):
                update(g, 0, t, rho)
            return carry

        lax.fori_loop(0, NT, last, 0)
        out_local(g).start()
        out_sib(g).start()

    half_copy(0, c).wait_send()
    for b in range(NB):
        v_y(b, y).wait_send()
        v_own(b, c).wait_send()
        v_fwd(b, c).wait_send()
        z_chunk(b // 4, b % 4, x).wait_send()
    for g in range(2):
        out_local(g).wait()
        out_sib(g).wait_send()
        out_from_sib(g).wait_recv()


def solution(mesh):
    def local_run(z_cols, v_local, t_local):
        f32 = jnp.float32
        t6 = t_local.reshape(NB, 4, 2, W, W).transpose(0, 2, 1, 3, 4)[:, :, :, :, None, :]
        same = jnp.eye(4, dtype=bool)[None, None, :, None, :, None]
        t0 = jnp.where(same, t6, 0.0).reshape(NB, 2, HALF, HALF)
        any_spec = pl.BlockSpec(memory_space=pl.ANY)
        dma = pltpu.SemaphoreType.DMA
        z_t = pl.pallas_call(
            _kernel,
            out_shape=jax.ShapeDtypeStruct((4 * HALF, ROWS), f32),
            in_specs=[any_spec] * 3,
            out_specs=any_spec,
            scratch_shapes=[
                pltpu.VMEM((2 * VT * TILE, TILE), f32),
                pltpu.VMEM((2, HALF, 2 * ROWS), f32),
                pltpu.VMEM((NB, 2, HALF, HALF), f32),
                pltpu.VMEM((2, HALF, TILE), f32),
                pltpu.VMEM((2, 2, HALF, TILE), f32),
                pltpu.VMEM((HALF, TILE), f32),
                pltpu.VMEM((HALF, TILE), f32),
                pltpu.VMEM((4, HALF, TILE), f32),
                pltpu.VMEM((2, TILE, TILE), f32),
                pltpu.VMEM((2, TILE, TILE), f32),
                *[dma((NB,))] * 9,
                dma((2,)), dma((2, 2)), dma, dma((4,)), dma, dma((2,)), dma((3,)), dma((2,)), dma((2,)),
            ],
            compiler_params=pltpu.CompilerParams(collective_id=0, has_side_effects=True, vmem_limit_bytes=63 * 2**20),
            name="backtransform",
        )(z_cols.T, v_local, t0)
        return z_t.T

    return jax.shard_map(
        local_run,
        mesh=mesh,
        in_specs=(P("kpt", ("col", "row")), P(("kpt", "row"), "col"), P("kpt", None, None)),
        out_specs=P(("kpt", "row"), "col"),
        check_vma=False,
    )
```

time: 8810 us -> 419 us (0.05)
  waiting for transfers between devices: 5090 us -> 0 us
  blocking collectives: 1790 us -> 0 us
  matrix products: 1720 us -> 0 us
  Pallas kernels: 0 us -> 391 us
  local copies, waits for them, and re-layouts: 145 us -> 25.6 us
    psum x192 -> x0, waiting for transfers between devices: 5060 us -> none  [panel_step(): s_full = lax.psum(s_part, 'row')]
    all_gather x96 -> x0, blocking collectives: 1790 us -> none  [group_step(): gathered = lax.all_gather(own_panel, 'col')]
    dot_general x576 -> x0, matrix products: 1720 us -> none  [the longest x192 825 us: panel_step(): jnp.dot(panel, w_full, precision=PRECISE, preferred_element_type=jnp.floa...]
    pallas_call x0 -> x1, Pallas kernels: none -> 391 us  [local_run(): pl.pallas_call(_kernel, out_shape=jax.ShapeDtypeStruct((4 * HALF, ROWS),...]
    dynamic_slice x96 -> x0, local copies, waits for them, and re-layouts: 135 us -> none  [group_step(): lax.dynamic_slice_in_dim(v_local, group_idx * panel_width, panel_width, a...]
  transfers between devices with their start and end apart: 193 -> 0, of which waited for: 193 -> 0; matrix products, arithmetic and copies ran while one was open for 0% -> 0% of each run, Pallas kernels for 0% -> 0%
where the time goes in v1:
time: 419 us; the launch traced here: 418 us
  Pallas kernels  391 us (93%)
  local copies, waits for them, and re-layouts  25.6 us (6%)
    pallas_call x1, Pallas kernels, local_run(): pl.pallas_call(_kernel, out_shape=jax.ShapeDtypeStruct((4 * HALF, ROWS),...  391 us
    broadcast_in_dim x4, local copies, waits for them, and re-layouts, local_run(): t0 = jnp.where(same, t6, 0.0).reshape(NB, 2, HALF, HALF)  15.2 us

profile of v1, /device:TPU:0, one launch (start us, length us, event | category | flops | bytes accessed | tf_op | source)
XLA Modules:
  0.0 418.5 jit_solution(17680918512045388913)
XLA Ops:
  0.0 2.9 copy.8
  3.0 0.4 copy.9
  3.3 5.8 %broadcast_in_dim.31 = f32[24,2,4,32,4,32]{5,4,3,2,1,0:T(4,128)} broadcast(f32[24,2,4,32,32]{4,3,2,1,0:T(8,128)S(1)} %copy.9), dimensions={0,1,2,3,5} | broadcast | bytes 3932160 | tf_op jit(solution)/shard_map/jit(_where)/broadcast_in_dim | solution.py:300
  9.1 9.2 %broadcast_in_dim.32 = f32[24,2,128,128]{3,2,1,0:T(8,128)S(1)} reshape(f32[24,2,4,32,4,32]{5,4,3,2,1,0:T(4,128)} %broadcast_in_dim.31) | data formatting | bytes 6291456 | tf_op jit(solution)/shard_map/jit(_where)/broadcast_in_dim | solution.py:300
  18.3 0.1 broadcast_in_dim.28
  18.4 0.1 broadcast_in_dim.29
  18.6 1.9 broadcast_select_fusion.t0_in
  20.5 3.5 copy.7
  24.1 390.9 %backtransform.1 = f32[512,1536]{1,0:T(8,128)} custom-call(f32[128,6144]{1,0:T(8,128)} %bitcast.6, f32[1536,3072]{1,0:T(8,128)} %v_in.1, f32[24,2,128,128]{3,2,1,0:T(8,128)} %broadcast_select_fusion.t0_in), custom_call_target="tpu_custom_call" | custom-call | tf_op jit(solution)/shard_map/backtransform/pallas_call | solution.py:303
  414.9 3.5 copy.10
  (1 shorter events, 0.0 us)

commit v2 on v1

v2 whole, which is shorter than its diff:
```python
import jax
import jax.numpy as jnp
from jax import lax
from jax.experimental import pallas as pl
from jax.experimental.pallas import tpu as pltpu
from jax.sharding import PartitionSpec as P

PRECISE = lax.Precision.HIGHEST
MESH = pl.DeviceIdType.MESH

W = 32
ROWS = 1536
TILE = 256
HALF = 128
NT = ROWS // TILE
NB = 24
VT = 4 * sum(range(1, NT + 1))
AHEAD = 12


def _dot(a, b, ca, cb):
    return lax.dot_general(a, b, (((ca,), (cb,)), ((), ())), precision=PRECISE, preferred_element_type=jnp.float32)


def _base(b):
    q, i = b // 4, b % 4
    return 4 * (NT * q - (q * (q - 1)) // 2) + i * (NT - q)


def _panel(idx):
    return jnp.where(idx < HALF, 2 * (idx // W), 2 * ((idx - HALF) // W) + 1)


def _pairs(lo, n, body):
    def two(h, carry):
        body(lo + 2 * h)
        body(lo + 2 * h + 1)
        return carry

    lax.fori_loop(0, n // 2, two, 0)

    @pl.when(n % 2 == 1)
    def _():
        body(lo + n - 1)


def _kernel(zt_in, v_in, tt_in, out, vbuf, vtr, zt, tt, acc, srecv, wbuf, usend, urecv, uhalf, ufull, tbuf,
            loc_sem, ys_sem, yr_sem, os_sem, or_sem, fs_sem, fr_sem, zs_sem, zr_sem,
            ss_sem, sr_sem, us_sem, ur_sem, hs_sem, hr_sem, ts_sem, tr_sem, tt_sem, zo_sem, out_sem, outs_sem, outr_sem):
    ridx = lax.axis_index("row")
    y = lax.axis_index("col")
    x, c = ridx // 2, ridx % 2
    xn = {"row": (ridx + 2) % 4}
    sib = {"row": ridx + 1 - 2 * c}
    yn = {"col": 1 - y}

    barrier = pltpu.get_barrier_semaphore()
    for dev in (xn, sib, yn):
        pl.semaphore_signal(barrier, inc=1, device_id=dev, device_id_type=MESH)

    def remote(src, dst, send, recv, dev):
        return pltpu.make_async_remote_copy(src, dst, send, recv, device_id=dev, device_id_type=MESH)

    def slab(b, rho, par):
        start = (rho * VT + _base(b)) * TILE + 64 * (b % 4)
        return vbuf.at[pl.ds(pl.multiple_of(start, 64), ROWS - 64 * b), pl.ds(pl.multiple_of(par * HALF, HALF), HALF)]

    def v_local(b):
        return pltpu.make_async_copy(v_in.at[pl.ds(64 * b, ROWS - 64 * b), pl.ds(HALF * b, HALF)], slab(b, c, y), loc_sem.at[b])

    def v_y(b, par):
        return remote(slab(b, c, par), slab(b, c, par), ys_sem.at[b], yr_sem.at[b], yn)

    def v_own(b, rho):
        return remote(slab(b, rho, y), slab(b, rho, y), os_sem.at[b], or_sem.at[b], sib)

    def v_fwd(b, rho):
        return remote(slab(b, rho, 1 - y), slab(b, rho, 1 - y), fs_sem.at[b], fr_sem.at[b], sib)

    def v_issue(b):
        v_local(b).wait()
        v_y(b, y).start()
        v_own(b, c).start()

    def static_block(b, fn):
        for qq in range(NT):

            @pl.when(b // 4 == qq)
            def _(qq=qq):
                for ii in range(4):

                    @pl.when(b % 4 == ii)
                    def _(ii=ii):
                        fn(4 * qq + ii)

    def z_own(t, rho):
        return pltpu.make_async_copy(
            zt_in.at[:, pl.ds(pl.multiple_of((2 * x + rho) * ROWS + t * TILE, TILE), TILE)],
            zt.at[x, :, pl.ds((2 * t + rho) * TILE, TILE)], zo_sem.at[2 * t + rho])

    def z_chunk(t, j, g):
        src = (2 * (1 - x) + j // 2) * ROWS + t * TILE + (j % 2) * HALF
        return remote(
            zt_in.at[:, pl.ds(pl.multiple_of(src, HALF), HALF)],
            zt.at[g, :, pl.ds(pl.multiple_of(2 * t * TILE + j * HALF, HALF), HALF)],
            zs_sem.at[4 * t + j], zr_sem.at[4 * t + j], xn)

    tt_copy = pltpu.make_async_copy(tt_in, tt, tt_sem)

    for b in range(NB - 1, NB - 5, -1):
        v_local(b).start()
    tt_copy.start()
    for t in range(NT - 1, -1, -1):
        for rho in range(2):
            z_own(t, rho).start()
    for b in range(NB - 5, -1, -1):
        v_local(b).start()
    for b in range(NB):
        if b % 4:
            for rho in range(2):
                vbuf[pl.ds((rho * VT + _base(b)) * TILE, 64 * (b % 4)), :] = jnp.zeros((64 * (b % 4), TILE), jnp.float32)

    pl.semaphore_wait(barrier, 3)
    for b in range(NB - 1, NB - 1 - AHEAD, -1):
        v_issue(b)
        if b == NB - 2:
            for j in range(4):
                z_chunk(NT - 1, j, x).start()
    for t in range(NT):
        for rho in range(2):
            z_own(t, rho).wait()
    tt_copy.wait()

    def rows(b, t, rho):
        return pl.ds(pl.multiple_of((rho * VT + _base(b) + t - b // 4) * TILE, TILE), TILE)

    def v_tile(b, t):
        return jnp.concatenate([vbuf[rows(b, t, rho), :] for rho in range(2)], axis=0)

    def cols(t):
        return pl.ds(pl.multiple_of(t * 2 * TILE, 2 * TILE), 2 * TILE)

    def s_copy(g, b):
        return remote(acc.at[g], srecv.at[g, b % 2], ss_sem.at[g], sr_sem.at[g, b % 2], xn)

    def weights(g, b):
        if g == 0:

            @pl.when(b % 2 != c)
            def _():
                t_copy(b).wait_recv()

        s_copy(g, b).wait_recv()
        s_sum = acc[g] + srecv[g, b % 2]
        wbuf[...] = _dot(s_sum, tbuf[b % 2], 1, 0)
        s_copy(g, b).wait_send()

    def update(g, b, t):
        if g == 0:
            v_tr = v_tile(b, t).T
            vtr[:, cols(t)] = v_tr
        else:
            v_tr = vtr[:, cols(t)]
        zt[g, :, cols(t)] = zt[g, :, cols(t)] - _dot(wbuf[...], v_tr, 1, 0)

    def partial_s(g, b, t):
        acc[g] += _dot(zt[g, :, cols(t)], v_tile(b, t), 1, 0)

    def sweep(g, k):
        @pl.when(k < NB - 1)
        def _():
            weights(g, k + 1)

        acc[g] = jnp.zeros((HALF, TILE), jnp.float32)
        first = (k + 1) // 4
        late = jnp.where(k % 4 == 3, 0, 1)

        @pl.when(late == 1)
        def _():
            update(g, k + 1, first)

        def both(t):
            partial_s(g, k, t - 1)
            update(g, k + 1, t)

        _pairs(first + late, NT - first - late, both)
        partial_s(g, k, NT - 1)
        s_copy(g, k).start()

    def u_copy(b):
        return remote(usend, urecv.at[b % 4], us_sem, ur_sem.at[b % 4], xn)

    half_copy = remote(uhalf, ufull.at[pl.ds(pl.multiple_of(c * HALF, HALF), HALF), :], hs_sem, hr_sem, sib)

    def t_copy(b):
        return remote(tbuf.at[b % 2], tbuf.at[b % 2], ts_sem, tr_sem.at[b % 2], sib)

    def gram(b):
        def tile(t):
            own = jnp.concatenate(
                [vbuf[rows(b, t, rho), pl.ds(pl.multiple_of(c * HALF, HALF), HALF)] for rho in range(2)], axis=0)
            usend[...] += _dot(own, v_tile(b, t), 0, 0)

        usend[...] = jnp.zeros((HALF, TILE), jnp.float32)
        _pairs(b // 4, NT - b // 4, tile)
        u_copy(b).start()

    def u_half(b):
        u_copy(b).wait()
        total = usend[...] + urecv[b % 4]
        pa = 2 * (lax.broadcasted_iota(jnp.int32, (HALF, TILE), 0) // W) + c
        pb = _panel(lax.broadcasted_iota(jnp.int32, (HALF, TILE), 1))
        half = jnp.where(pa < pb, total, 0.0)

        @pl.when(b % 2 == c)
        def _():
            ufull[pl.ds(pl.multiple_of(c * HALF, HALF), HALF), :] = half

        @pl.when(b % 2 != c)
        def _():
            @pl.when(b < NB - 2)
            def _():
                half_copy.wait_send()

            uhalf[...] = half
            half_copy.start()

    def merge(b):
        half_copy.wait_recv()
        u_all = ufull[...]
        slot = b % 2

        @pl.when(b < NB - 2)
        def _():
            t_copy(b).wait_send()

        same = (lax.broadcasted_iota(jnp.int32, (HALF, HALF), 0) // W) == (lax.broadcasted_iota(jnp.int32, (HALF, HALF), 1) // W)

        def diagonal(par):
            stack = jnp.concatenate([tt[8 * b + 2 * i + par] for i in range(4)], axis=0)
            return jnp.where(same, jnp.concatenate([stack] * 4, axis=1), 0.0)

        even, odd = diagonal(0), diagonal(1)
        pairs = jnp.where(same, u_all[:HALF, HALF:], 0.0)
        tbuf[slot, :HALF, :HALF] = even
        tbuf[slot, :HALF, HALF:] = jnp.zeros((HALF, HALF), jnp.float32)
        tbuf[slot, HALF:, :HALF] = -_dot(_dot(odd, pairs, 1, 1), even, 1, 0)
        tbuf[slot, HALF:, HALF:] = odd
        pa = _panel(lax.broadcasted_iota(jnp.int32, (TILE, TILE), 0))
        pb = _panel(lax.broadcasted_iota(jnp.int32, (TILE, TILE), 1))
        for size in (2, 4):
            level = (pa // (2 * size) == pb // (2 * size)) & (pa // size < pb // size)
            t_now = tbuf[slot]
            tbuf[slot] = t_now - _dot(_dot(t_now, jnp.where(level, u_all, 0.0), 1, 1), t_now, 1, 0)
        t_copy(b).start()

    def step(s, carry):
        k = NB + 2 - s

        @pl.when(k < NB)
        def _():
            @pl.when(k % 4 == 3)
            def _():
                for j in range(4):
                    z_chunk(k // 4, j, 1 - x).wait_recv()

            sweep(0, k)
            sweep(1, k)

            @pl.when(k >= AHEAD)
            def _():
                static_block(k - AHEAD, v_issue)

        @pl.when((k >= 6) & (k < NB + 2))
        def _():
            z_chunk((k - 6) // 4, 3 - (k - 6) % 4, x).start()

        @pl.when((k >= 1) & (k <= NB))
        def _():
            u_half(k - 1)

        @pl.when(k >= 3)
        def _():
            def forward(b):
                v_y(b, 1 - y).wait_recv()
                v_fwd(b, c).start()

            static_block(k - 3, forward)

        @pl.when((k >= 2) & (k < NB + 2))
        def _():
            def arrived(b):
                v_own(b, 1 - c).wait_recv()
                v_fwd(b, 1 - c).wait_recv()

            static_block(k - 2, arrived)
            gram(k - 2)

        @pl.when((k >= 1) & (k <= NB) & ((k - 1) % 2 == c))
        def _():
            merge(k - 1)

        return carry

    lax.fori_loop(0, NB + 3, step, 0)

    def out_rows(g):
        return pl.ds(pl.multiple_of((2 * g + c) * HALF, HALF), HALF)

    def out_cols(t):
        return pl.ds(t * TILE, TILE)

    def out_local(g, t):
        return pltpu.make_async_copy(
            zt.at[g, :, pl.ds(pl.multiple_of((2 * t + c) * TILE, TILE), TILE)], out.at[out_rows(g), out_cols(t)],
            out_sem.at[g * NT + t])

    def out_sib(g, t):
        return remote(
            zt.at[g, :, pl.ds(pl.multiple_of((2 * t + 1 - c) * TILE, TILE), TILE)], out.at[out_rows(g), out_cols(t)],
            outs_sem.at[g * NT + t], outr_sem.at[g * NT + t], sib)

    def out_from_sib(g, t):
        part = out.at[pl.ds(pl.multiple_of((2 * g + 1 - c) * HALF, HALF), HALF), out_cols(t)]
        return remote(part, part, outs_sem.at[g * NT + t], outr_sem.at[g * NT + t], sib)

    for g in range(2):
        weights(g, 0)
        _pairs(0, NT, lambda t, g=g: update(g, 0, t))
        for t in range(NT):
            out_local(g, t).start()
            out_sib(g, t).start()

    half_copy.wait_send()
    t_copy(0).wait_send()
    for b in range(NB):
        v_y(b, y).wait_send()
        v_own(b, c).wait_send()
        v_fwd(b, c).wait_send()
        z_chunk(b // 4, b % 4, x).wait_send()
    for g in range(2):
        for t in range(NT):
            out_local(g, t).wait()
            out_sib(g, t).wait_send()
            out_from_sib(g, t).wait_recv()


def solution(mesh):
    def local_run(z_cols, v_local, t_local):
        f32 = jnp.float32
        any_spec = pl.BlockSpec(memory_space=pl.ANY)
        dma = pltpu.SemaphoreType.DMA
        z_t = pl.pallas_call(
            _kernel,
            out_shape=jax.ShapeDtypeStruct((4 * HALF, ROWS), f32),
            in_specs=[any_spec] * 3,
            out_specs=any_spec,
            scratch_shapes=[
                pltpu.VMEM((2 * VT * TILE, TILE), f32),
                pltpu.VMEM((TILE, 2 * ROWS), f32),
                pltpu.VMEM((2, HALF, 2 * ROWS), f32),
                pltpu.VMEM((NB * 8, W, W), f32),
                pltpu.VMEM((2, HALF, TILE), f32),
                pltpu.VMEM((2, 2, HALF, TILE), f32),
                pltpu.VMEM((HALF, TILE), f32),
                pltpu.VMEM((HALF, TILE), f32),
                pltpu.VMEM((4, HALF, TILE), f32),
                pltpu.VMEM((HALF, TILE), f32),
                pltpu.VMEM((TILE, TILE), f32),
                pltpu.VMEM((2, TILE, TILE), f32),
                *[dma((NB,))] * 9,
                dma((2,)), dma((2, 2)), dma, dma((4,)), dma, dma, dma, dma((2,)), dma, *[dma((2 * NT,))] * 4,
            ],
            compiler_params=pltpu.CompilerParams(collective_id=0, has_side_effects=True, vmem_limit_bytes=63 * 2**20),
            name="backtransform",
        )(z_cols.T, v_local, t_local.transpose(0, 2, 1))
        return z_t.T

    return jax.shard_map(
        local_run,
        mesh=mesh,
        in_specs=(P("kpt", ("col", "row")), P(("kpt", "row"), "col"), P("kpt", None, None)),
        out_specs=P(("kpt", "row"), "col"),
        check_vma=False,
    )
```

time: 419 us -> 284 us (0.68)
  Pallas kernels: 391 us -> 274 us
  local copies, waits for them, and re-layouts: 25.6 us -> 10.1 us
    pallas_call x1, Pallas kernels: 391 us -> 274 us  [local_run(): pl.pallas_call(_kernel, out_shape=jax.ShapeDtypeStruct((4 * HALF, ROWS),...]
    broadcast_in_dim x4 -> x0, local copies, waits for them, and re-layouts: 15.2 us -> none  [local_run(): t0 = jnp.where(same, t6, 0.0).reshape(NB, 2, HALF, HALF)]
where the time goes in v2:
time: 284 us
  Pallas kernels  274 us (96%)
  local copies, waits for them, and re-layouts  10.1 us (4%)
    pallas_call x1, Pallas kernels, local_run(): pl.pallas_call(_kernel, out_shape=jax.ShapeDtypeStruct((4 * HALF, ROWS),...  274 us
    unnamed x4, local copies, waits for them, and re-layouts  6.58 us

profile of v2, /device:TPU:0, one launch (start us, length us, event | category | flops | bytes accessed | tf_op | source)
XLA Modules:
  0.0 283.7 jit_solution(12725773331672878296)
XLA Ops:
  0.0 0.0 copy-start
  0.0 3.6 %copy.4 = f32[6144,128]{0,1:T(8,128)} copy(f32[6144,128]{1,0:T(8,128)} %param.3) | data formatting | bytes 6291456 | tf_op args[0]
  3.6 0.0 copy-done
  3.6 2.9 %copy.5 = f32[192,32,32]{1,2,0:T(8,128)} copy(f32[192,32,32]{0,2,1:T(8,128)S(1)} %copy-done) | data formatting | bytes 1572864 | tf_op args[2]
  6.6 273.5 %backtransform.1 = f32[512,1536]{1,0:T(8,128)} custom-call(f32[128,6144]{1,0:T(8,128)} %bitcast.4, f32[1536,3072]{1,0:T(8,128)} %v_in.1, f32[192,32,32]{2,1,0:T(8,128)} %bitcast.5), custom_call_target="tpu_custom_call" | custom-call | tf_op jit(solution)/shard_map/backtransform/pallas_call | solution.py:353
  280.1 3.5 %copy.6 = f32[1536,512]{1,0:T(8,128)} copy(f32[1536,512]{0,1:T(8,128)} %bitcast.3) | data formatting | bytes 6291456 | tf_op jit(solution)/shard_map/transpose | solution.py:377
Async XLA Ops:
  0.0 3.6 %copy-start = (f32[192,32,32]{0,2,1:T(8,128)S(1)}, f32[192,32,32]{0,2,1:T(8,128)}, u32[]{:S(2)}) copy-start(f32[192,32,32]{0,2,1:T(8,128)} %param.5) | copy-start | bytes 2359300

commit v3 on v2

--- a/solution.py
+++ b/solution.py
@@ -44,7 +44,7 @@
         body(lo + n - 1)
 
 
-def _kernel(zt_in, v_in, tt_in, out, vbuf, vtr, zt, tt, acc, srecv, wbuf, usend, urecv, uhalf, ufull, tbuf,
+def _kernel(zt_in, v_in, tt_in, out, vbuf, vtr, zt, tt, acc, srecv, wbuf, gacc, usend, urecv, uhalf, upack, tbuf,
             loc_sem, ys_sem, yr_sem, os_sem, or_sem, fs_sem, fr_sem, zs_sem, zr_sem,
             ss_sem, sr_sem, us_sem, ur_sem, hs_sem, hr_sem, ts_sem, tr_sem, tt_sem, zo_sem, out_sem, outs_sem, outr_sem):
     ridx = lax.axis_index("row")
@@ -187,10 +187,13 @@
         partial_s(g, k, NT - 1)
         s_copy(g, k).start()
 
+    ra = lax.broadcasted_iota(jnp.int32, (HALF, HALF), 0) // W
+    rb = lax.broadcasted_iota(jnp.int32, (HALF, HALF), 1) // W
+
     def u_copy(b):
-        return remote(usend, urecv.at[b % 4], us_sem, ur_sem.at[b % 4], xn)
-
-    half_copy = remote(uhalf, ufull.at[pl.ds(pl.multiple_of(c * HALF, HALF), HALF), :], hs_sem, hr_sem, sib)
+        return remote(usend.at[b % 2], urecv.at[b % 4], us_sem.at[b % 2], ur_sem.at[b % 4], xn)
+
+    half_copy = remote(uhalf, upack.at[c], hs_sem, hr_sem, sib)
 
     def t_copy(b):
         return remote(tbuf.at[b % 2], tbuf.at[b % 2], ts_sem, tr_sem.at[b % 2], sib)
@@ -199,22 +202,24 @@
         def tile(t):
             own = jnp.concatenate(
                 [vbuf[rows(b, t, rho), pl.ds(pl.multiple_of(c * HALF, HALF), HALF)] for rho in range(2)], axis=0)
-            usend[...] += _dot(own, v_tile(b, t), 0, 0)
-
-        usend[...] = jnp.zeros((HALF, TILE), jnp.float32)
+            gacc[...] += _dot(own, v_tile(b, t), 0, 0)
+
+        gacc[...] = jnp.zeros((HALF, TILE), jnp.float32)
         _pairs(b // 4, NT - b // 4, tile)
+
+        def cols_of(par):
+            return gacc[:, pl.ds(pl.multiple_of(par * HALF, HALF), HALF)]
+
+        usend[b % 2] = jnp.where(ra <= rb, cols_of(1 - c), cols_of(c))
         u_copy(b).start()
 
     def u_half(b):
         u_copy(b).wait()
-        total = usend[...] + urecv[b % 4]
-        pa = 2 * (lax.broadcasted_iota(jnp.int32, (HALF, TILE), 0) // W) + c
-        pb = _panel(lax.broadcasted_iota(jnp.int32, (HALF, TILE), 1))
-        half = jnp.where(pa < pb, total, 0.0)
+        total = usend[b % 2] + urecv[b % 4]
 
         @pl.when(b % 2 == c)
         def _():
-            ufull[pl.ds(pl.multiple_of(c * HALF, HALF), HALF), :] = half
+            upack[c] = total
 
         @pl.when(b % 2 != c)
         def _():
@@ -222,36 +227,40 @@
             def _():
                 half_copy.wait_send()
 
-            uhalf[...] = half
+            uhalf[...] = total
             half_copy.start()
 
     def merge(b):
         half_copy.wait_recv()
-        u_all = ufull[...]
         slot = b % 2
 
         @pl.when(b < NB - 2)
         def _():
             t_copy(b).wait_send()
 
-        same = (lax.broadcasted_iota(jnp.int32, (HALF, HALF), 0) // W) == (lax.broadcasted_iota(jnp.int32, (HALF, HALF), 1) // W)
+        same = ra == rb
 
         def diagonal(par):
             stack = jnp.concatenate([tt[8 * b + 2 * i + par] for i in range(4)], axis=0)
             return jnp.where(same, jnp.concatenate([stack] * 4, axis=1), 0.0)
 
+        even_part, odd_part = upack[0], upack[1]
+        eo = jnp.where(ra <= rb, even_part, 0.0).T
+        u_tr = jnp.concatenate([
+            jnp.concatenate([jnp.where(ra > rb, even_part, 0.0), jnp.where(ra < rb, odd_part, 0.0).T], axis=1),
+            jnp.concatenate([eo, jnp.where(ra > rb, odd_part, 0.0)], axis=1)], axis=0)
         even, odd = diagonal(0), diagonal(1)
-        pairs = jnp.where(same, u_all[:HALF, HALF:], 0.0)
+        pairs = jnp.where(same, eo, 0.0)
         tbuf[slot, :HALF, :HALF] = even
         tbuf[slot, :HALF, HALF:] = jnp.zeros((HALF, HALF), jnp.float32)
-        tbuf[slot, HALF:, :HALF] = -_dot(_dot(odd, pairs, 1, 1), even, 1, 0)
+        tbuf[slot, HALF:, :HALF] = -_dot(_dot(odd, pairs, 1, 0), even, 1, 0)
         tbuf[slot, HALF:, HALF:] = odd
         pa = _panel(lax.broadcasted_iota(jnp.int32, (TILE, TILE), 0))
         pb = _panel(lax.broadcasted_iota(jnp.int32, (TILE, TILE), 1))
         for size in (2, 4):
-            level = (pa // (2 * size) == pb // (2 * size)) & (pa // size < pb // size)
+            level = (pa // (2 * size) == pb // (2 * size)) & (pa // size > pb // size)
             t_now = tbuf[slot]
-            tbuf[slot] = t_now - _dot(_dot(t_now, jnp.where(level, u_all, 0.0), 1, 1), t_now, 1, 0)
+            tbuf[slot] = t_now - _dot(_dot(t_now, jnp.where(level, u_tr, 0.0), 1, 0), t_now, 1, 0)
         t_copy(b).start()
 
     def step(s, carry):
@@ -271,11 +280,7 @@
             def _():
                 static_block(k - AHEAD, v_issue)
 
-        @pl.when((k >= 6) & (k < NB + 2))
-        def _():
-            z_chunk((k - 6) // 4, 3 - (k - 6) % 4, x).start()
-
-        @pl.when((k >= 1) & (k <= NB))
+        @pl.when((k >= 1) & (k <= NB) & ((k - 1) % 2 != c))
         def _():
             u_half(k - 1)
 
@@ -296,8 +301,13 @@
             static_block(k - 2, arrived)
             gram(k - 2)
 
+        @pl.when((k >= 6) & (k < NB + 2))
+        def _():
+            z_chunk((k - 6) // 4, 3 - (k - 6) % 4, x).start()
+
         @pl.when((k >= 1) & (k <= NB) & ((k - 1) % 2 == c))
         def _():
+            u_half(k - 1)
             merge(k - 1)
 
         return carry
@@ -364,12 +374,13 @@
                 pltpu.VMEM((2, 2, HALF, TILE), f32),
                 pltpu.VMEM((HALF, TILE), f32),
                 pltpu.VMEM((HALF, TILE), f32),
-                pltpu.VMEM((4, HALF, TILE), f32),
-                pltpu.VMEM((HALF, TILE), f32),
-                pltpu.VMEM((TILE, TILE), f32),
+                pltpu.VMEM((2, HALF, HALF), f32),
+                pltpu.VMEM((4, HALF, HALF), f32),
+                pltpu.VMEM((HALF, HALF), f32),
+                pltpu.VMEM((2, HALF, HALF), f32),
                 pltpu.VMEM((2, TILE, TILE), f32),
                 *[dma((NB,))] * 9,
-                dma((2,)), dma((2, 2)), dma, dma((4,)), dma, dma, dma, dma((2,)), dma, *[dma((2 * NT,))] * 4,
+                dma((2,)), dma((2, 2)), dma((2,)), dma((4,)), dma, dma, dma, dma((2,)), dma, *[dma((2 * NT,))] * 4,
             ],
             compiler_params=pltpu.CompilerParams(collective_id=0, has_side_effects=True, vmem_limit_bytes=63 * 2**20),
             name="backtransform",

time: 284 us -> 276 us (0.972)
  Pallas kernels: 274 us -> 265 us
    pallas_call x1, Pallas kernels: 274 us -> 265 us  [local_run(): pl.pallas_call(_kernel, out_shape=jax.ShapeDtypeStruct((4 * HALF, ROWS),...]
where the time goes in v3:
time: 276 us; the launch traced here: 275 us
  Pallas kernels  265 us (96%)
  local copies, waits for them, and re-layouts  10.1 us (4%)
    pallas_call x1, Pallas kernels, local_run(): pl.pallas_call(_kernel, out_shape=jax.ShapeDtypeStruct((4 * HALF, ROWS),...  265 us
    unnamed x4, local copies, waits for them, and re-layouts  6.58 us

profile of v3, /device:TPU:0, one launch (start us, length us, event | category | flops | bytes accessed | tf_op | source)
XLA Modules:
  0.0 275.4 jit_solution(17304706796741385102)
XLA Ops:
  0.0 0.0 copy-start
  0.0 3.6 %copy.4 = f32[6144,128]{0,1:T(8,128)} copy(f32[6144,128]{1,0:T(8,128)} %param.3) | data formatting | bytes 6291456 | tf_op args[0]
  3.6 0.0 copy-done
  3.6 2.9 %copy.5 = f32[192,32,32]{1,2,0:T(8,128)} copy(f32[192,32,32]{0,2,1:T(8,128)S(1)} %copy-done) | data formatting | bytes 1572864 | tf_op args[2]
  6.6 265.3 %backtransform.1 = f32[512,1536]{1,0:T(8,128)} custom-call(f32[128,6144]{1,0:T(8,128)} %bitcast.4, f32[1536,3072]{1,0:T(8,128)} %v_in.1, f32[192,32,32]{2,1,0:T(8,128)} %bitcast.5), custom_call_target="tpu_custom_call" | custom-call | tf_op jit(solution)/shard_map/backtransform/pallas_call | solution.py:363
  271.9 3.5 %copy.6 = f32[1536,512]{1,0:T(8,128)} copy(f32[1536,512]{0,1:T(8,128)} %bitcast.3) | data formatting | bytes 6291456 | tf_op jit(solution)/shard_map/transpose | solution.py:388
Async XLA Ops:
  0.0 3.6 %copy-start = (f32[192,32,32]{0,2,1:T(8,128)S(1)}, f32[192,32,32]{0,2,1:T(8,128)}, u32[]{:S(2)}) copy-start(f32[192,32,32]{0,2,1:T(8,128)} %param.5) | copy-start | bytes 2359300

commit v4 on v3

--- a/solution.py
+++ b/solution.py
@@ -152,7 +152,7 @@
 
         s_copy(g, b).wait_recv()
         s_sum = acc[g] + srecv[g, b % 2]
-        wbuf[...] = _dot(s_sum, tbuf[b % 2], 1, 0)
+        wbuf[...] = _dot(s_sum, tbuf[b % 4], 1, 0)
         s_copy(g, b).wait_send()
 
     def update(g, b, t):
@@ -196,7 +196,7 @@
     half_copy = remote(uhalf, upack.at[c], hs_sem, hr_sem, sib)
 
     def t_copy(b):
-        return remote(tbuf.at[b % 2], tbuf.at[b % 2], ts_sem, tr_sem.at[b % 2], sib)
+        return remote(tbuf.at[b % 4], tbuf.at[b % 4], ts_sem, tr_sem.at[b % 4], sib)
 
     def gram(b):
         def tile(t):
@@ -232,7 +232,7 @@
 
     def merge(b):
         half_copy.wait_recv()
-        slot = b % 2
+        slot = b % 4
 
         @pl.when(b < NB - 2)
         def _():
@@ -264,35 +264,40 @@
         t_copy(b).start()
 
     def step(s, carry):
-        k = NB + 2 - s
-
-        @pl.when(k < NB)
-        def _():
-            @pl.when(k % 4 == 3)
+        k = NB + 1 - s
+        b_sweep = jnp.where(k == NB, NB - 1, k)
+        sweeps = (k < NB - 1) | (k == NB)
+
+        @pl.when(sweeps)
+        def _():
+            @pl.when(b_sweep % 4 == 3)
             def _():
                 for j in range(4):
-                    z_chunk(k // 4, j, 1 - x).wait_recv()
-
-            sweep(0, k)
-            sweep(1, k)
-
-            @pl.when(k >= AHEAD)
-            def _():
-                static_block(k - AHEAD, v_issue)
-
-        @pl.when((k >= 1) & (k <= NB) & ((k - 1) % 2 != c))
-        def _():
-            u_half(k - 1)
-
-        @pl.when(k >= 3)
+                    z_chunk(b_sweep // 4, j, 1 - x).wait_recv()
+
+            sweep(0, b_sweep)
+
+        @pl.when(k >= 2)
         def _():
             def forward(b):
                 v_y(b, 1 - y).wait_recv()
                 v_fwd(b, c).start()
 
-            static_block(k - 3, forward)
-
-        @pl.when((k >= 2) & (k < NB + 2))
+            static_block(k - 2, forward)
+
+        @pl.when((k >= 1) & (k <= NB) & ((k - 1) % 2 != c))
+        def _():
+            u_half(k - 1)
+
+        @pl.when(sweeps)
+        def _():
+            sweep(1, b_sweep)
+
+        @pl.when((k >= AHEAD) & (k < NB))
+        def _():
+            static_block(k - AHEAD, v_issue)
+
+        @pl.when(k >= 2)
         def _():
             def arrived(b):
                 v_own(b, 1 - c).wait_recv()
@@ -301,18 +306,20 @@
             static_block(k - 2, arrived)
             gram(k - 2)
 
-        @pl.when((k >= 6) & (k < NB + 2))
+        @pl.when(k >= 6)
         def _():
             z_chunk((k - 6) // 4, 3 - (k - 6) % 4, x).start()
 
-        @pl.when((k >= 1) & (k <= NB) & ((k - 1) % 2 == c))
-        def _():
-            u_half(k - 1)
-            merge(k - 1)
+        b_merge = jnp.where(k == 0, 0, k - 1)
+
+        @pl.when((k != 1) & (k <= NB) & (b_merge % 2 == c))
+        def _():
+            u_half(b_merge)
+            merge(b_merge)
 
         return carry
 
-    lax.fori_loop(0, NB + 3, step, 0)
+    lax.fori_loop(0, NB + 2, step, 0)
 
     def out_rows(g):
         return pl.ds(pl.multiple_of((2 * g + c) * HALF, HALF), HALF)
@@ -378,9 +385,9 @@
                 pltpu.VMEM((4, HALF, HALF), f32),
                 pltpu.VMEM((HALF, HALF), f32),
                 pltpu.VMEM((2, HALF, HALF), f32),
-                pltpu.VMEM((2, TILE, TILE), f32),
+                pltpu.VMEM((4, TILE, TILE), f32),
                 *[dma((NB,))] * 9,
-                dma((2,)), dma((2, 2)), dma((2,)), dma((4,)), dma, dma, dma, dma((2,)), dma, *[dma((2 * NT,))] * 4,
+                dma((2,)), dma((2, 2)), dma((2,)), dma((4,)), dma, dma, dma, dma((4,)), dma, *[dma((2 * NT,))] * 4,
             ],
             compiler_params=pltpu.CompilerParams(collective_id=0, has_side_effects=True, vmem_limit_bytes=63 * 2**20),
             name="backtransform",

time: 276 us -> 264 us (0.957)
  Pallas kernels: 265 us -> 254 us
    pallas_call x1, Pallas kernels: 265 us -> 254 us  [local_run(): pl.pallas_call(_kernel, out_shape=jax.ShapeDtypeStruct((4 * HALF, ROWS),...]
where the time goes in v4:
time: 264 us
  Pallas kernels  254 us (96%)
  local copies, waits for them, and re-layouts  10.1 us (4%)
    pallas_call x1, Pallas kernels, local_run(): pl.pallas_call(_kernel, out_shape=jax.ShapeDtypeStruct((4 * HALF, ROWS),...  254 us
    unnamed x4, local copies, waits for them, and re-layouts  6.58 us

profile of v4, /device:TPU:0, one launch (start us, length us, event | category | flops | bytes accessed | tf_op | source)
XLA Modules:
  0.0 263.8 jit_solution(9912708383235622926)
XLA Ops:
  0.0 0.0 copy-start
  0.0 3.6 %copy.4 = f32[6144,128]{0,1:T(8,128)} copy(f32[6144,128]{1,0:T(8,128)} %param.3) | data formatting | bytes 6291456 | tf_op args[0]
  3.6 0.0 copy-done
  3.6 2.9 %copy.5 = f32[192,32,32]{1,2,0:T(8,128)} copy(f32[192,32,32]{0,2,1:T(8,128)S(1)} %copy-done) | data formatting | bytes 1572864 | tf_op args[2]
  6.6 253.7 %backtransform.1 = f32[512,1536]{1,0:T(8,128)} custom-call(f32[128,6144]{1,0:T(8,128)} %bitcast.4, f32[1536,3072]{1,0:T(8,128)} %v_in.1, f32[192,32,32]{2,1,0:T(8,128)} %bitcast.5), custom_call_target="tpu_custom_call" | custom-call | tf_op jit(solution)/shard_map/backtransform/pallas_call | solution.py:370
  260.3 3.5 %copy.6 = f32[1536,512]{1,0:T(8,128)} copy(f32[1536,512]{0,1:T(8,128)} %bitcast.3) | data formatting | bytes 6291456 | tf_op jit(solution)/shard_map/transpose | solution.py:395
Async XLA Ops:
  0.0 3.6 %copy-start = (f32[192,32,32]{0,2,1:T(8,128)S(1)}, f32[192,32,32]{0,2,1:T(8,128)}, u32[]{:S(2)}) copy-start(f32[192,32,32]{0,2,1:T(8,128)} %param.5) | copy-start | bytes 2359300

commit v5 on v4

--- a/solution.py
+++ b/solution.py
@@ -44,7 +44,7 @@
         body(lo + n - 1)
 
 
-def _kernel(zt_in, v_in, tt_in, out, vbuf, vtr, zt, tt, acc, srecv, wbuf, gacc, usend, urecv, uhalf, upack, tbuf,
+def _kernel(z_in, v_in, t_in, out, vbuf, vtr, zt, zst, t_raw, tt, acc, srecv, wbuf, gacc, usend, urecv, uhalf, upack, tbuf,
             loc_sem, ys_sem, yr_sem, os_sem, or_sem, fs_sem, fr_sem, zs_sem, zr_sem,
             ss_sem, sr_sem, us_sem, ur_sem, hs_sem, hr_sem, ts_sem, tr_sem, tt_sem, zo_sem, out_sem, outs_sem, outr_sem):
     ridx = lax.axis_index("row")
@@ -95,21 +95,21 @@
 
     def z_own(t, rho):
         return pltpu.make_async_copy(
-            zt_in.at[:, pl.ds(pl.multiple_of((2 * x + rho) * ROWS + t * TILE, TILE), TILE)],
-            zt.at[x, :, pl.ds((2 * t + rho) * TILE, TILE)], zo_sem.at[2 * t + rho])
+            z_in.at[pl.ds(pl.multiple_of((2 * x + rho) * ROWS + t * TILE, TILE), TILE), :],
+            zst.at[x, t, pl.ds(rho * TILE, TILE), :], zo_sem.at[2 * t + rho])
 
     def z_chunk(t, j, g):
         src = (2 * (1 - x) + j // 2) * ROWS + t * TILE + (j % 2) * HALF
         return remote(
-            zt_in.at[:, pl.ds(pl.multiple_of(src, HALF), HALF)],
-            zt.at[g, :, pl.ds(pl.multiple_of(2 * t * TILE + j * HALF, HALF), HALF)],
+            z_in.at[pl.ds(pl.multiple_of(src, HALF), HALF), :],
+            zst.at[g, t, pl.ds(pl.multiple_of(j * HALF, HALF), HALF), :],
             zs_sem.at[4 * t + j], zr_sem.at[4 * t + j], xn)
 
-    tt_copy = pltpu.make_async_copy(tt_in, tt, tt_sem)
+    t_copy_in = pltpu.make_async_copy(t_in, t_raw, tt_sem)
 
     for b in range(NB - 1, NB - 5, -1):
         v_local(b).start()
-    tt_copy.start()
+    t_copy_in.start()
     for t in range(NT - 1, -1, -1):
         for rho in range(2):
             z_own(t, rho).start()
@@ -129,7 +129,13 @@
     for t in range(NT):
         for rho in range(2):
             z_own(t, rho).wait()
-    tt_copy.wait()
+    t_copy_in.wait()
+
+    def t_row(i, carry):
+        tt[pl.ds(i, NB * 8, stride=W), :] = t_raw[i].T
+        return carry
+
+    lax.fori_loop(0, W, t_row, 0)
 
     def rows(b, t, rho):
         return pl.ds(pl.multiple_of((rho * VT + _base(b) + t - b // 4) * TILE, TILE), TILE)
@@ -241,8 +247,9 @@
         same = ra == rb
 
         def diagonal(par):
-            stack = jnp.concatenate([tt[8 * b + 2 * i + par] for i in range(4)], axis=0)
-            return jnp.where(same, jnp.concatenate([stack] * 4, axis=1), 0.0)
+            at = [pl.multiple_of((8 * b + 2 * i + par) * W, W) for i in range(4)]
+            stack = jnp.concatenate([tt[pl.ds(row, W), :] for row in at], axis=0)
+            return jnp.where(same, jnp.concatenate([stack] * 4, axis=1), 0.0).T
 
         even_part, odd_part = upack[0], upack[1]
         eo = jnp.where(ra <= rb, even_part, 0.0).T
@@ -274,6 +281,8 @@
             def _():
                 for j in range(4):
                     z_chunk(b_sweep // 4, j, 1 - x).wait_recv()
+                for g in range(2):
+                    zt[g, :, cols(b_sweep // 4)] = zst[g, b_sweep // 4].T
 
             sweep(0, b_sweep)
 
@@ -321,29 +330,30 @@
 
     lax.fori_loop(0, NB + 2, step, 0)
 
-    def out_rows(g):
-        return pl.ds(pl.multiple_of((2 * g + c) * HALF, HALF), HALF)
-
-    def out_cols(t):
-        return pl.ds(t * TILE, TILE)
+    def out_part(g, t, core):
+        return out.at[pl.ds(t * TILE, TILE), pl.ds(pl.multiple_of((2 * g + core) * HALF, HALF), HALF)]
+
+    def z_part(g, t, rho):
+        return zst.at[g, t, pl.ds(pl.multiple_of(rho * TILE, TILE), TILE), :]
 
     def out_local(g, t):
-        return pltpu.make_async_copy(
-            zt.at[g, :, pl.ds(pl.multiple_of((2 * t + c) * TILE, TILE), TILE)], out.at[out_rows(g), out_cols(t)],
-            out_sem.at[g * NT + t])
+        return pltpu.make_async_copy(z_part(g, t, c), out_part(g, t, c), out_sem.at[g * NT + t])
 
     def out_sib(g, t):
-        return remote(
-            zt.at[g, :, pl.ds(pl.multiple_of((2 * t + 1 - c) * TILE, TILE), TILE)], out.at[out_rows(g), out_cols(t)],
-            outs_sem.at[g * NT + t], outr_sem.at[g * NT + t], sib)
+        return remote(z_part(g, t, 1 - c), out_part(g, t, c), outs_sem.at[g * NT + t], outr_sem.at[g * NT + t], sib)
 
     def out_from_sib(g, t):
-        part = out.at[pl.ds(pl.multiple_of((2 * g + 1 - c) * HALF, HALF), HALF), out_cols(t)]
+        part = out_part(g, t, 1 - c)
         return remote(part, part, outs_sem.at[g * NT + t], outr_sem.at[g * NT + t], sib)
 
     for g in range(2):
         weights(g, 0)
-        _pairs(0, NT, lambda t, g=g: update(g, 0, t))
+
+        def last(t, g=g):
+            update(g, 0, t)
+            zst[g, t] = zt[g, :, cols(t)].T
+
+        _pairs(0, NT, last)
         for t in range(NT):
             out_local(g, t).start()
             out_sib(g, t).start()
@@ -367,16 +377,18 @@
         f32 = jnp.float32
         any_spec = pl.BlockSpec(memory_space=pl.ANY)
         dma = pltpu.SemaphoreType.DMA
-        z_t = pl.pallas_call(
+        return pl.pallas_call(
             _kernel,
-            out_shape=jax.ShapeDtypeStruct((4 * HALF, ROWS), f32),
+            out_shape=jax.ShapeDtypeStruct((ROWS, 4 * HALF), f32),
             in_specs=[any_spec] * 3,
             out_specs=any_spec,
             scratch_shapes=[
                 pltpu.VMEM((2 * VT * TILE, TILE), f32),
                 pltpu.VMEM((TILE, 2 * ROWS), f32),
                 pltpu.VMEM((2, HALF, 2 * ROWS), f32),
-                pltpu.VMEM((NB * 8, W, W), f32),
+                pltpu.VMEM((2, NT, 2 * TILE, HALF), f32),
+                pltpu.VMEM((W, W, NB * 8), f32),
+                pltpu.VMEM((NB * 8 * W, W), f32),
                 pltpu.VMEM((2, HALF, TILE), f32),
                 pltpu.VMEM((2, 2, HALF, TILE), f32),
                 pltpu.VMEM((HALF, TILE), f32),
@@ -391,8 +403,7 @@
             ],
             compiler_params=pltpu.CompilerParams(collective_id=0, has_side_effects=True, vmem_limit_bytes=63 * 2**20),
             name="backtransform",
-        )(z_cols.T, v_local, t_local.transpose(0, 2, 1))
-        return z_t.T
+        )(z_cols, v_local, t_local.transpose(1, 2, 0))
 
     return jax.shard_map(
         local_run,

time: 264 us -> 260 us (0.985)
  local copies, waits for them, and re-layouts: 10.1 us -> 3.86 us
    transpose x1 -> x0, local copies, waits for them, and re-layouts: 3.55 us -> none  [local_run(): return z_t.T]
    unnamed x4 -> x1, local copies, waits for them, and re-layouts: 6.58 us -> 3.86 us
where the time goes in v5:
time: 260 us
  Pallas kernels  256 us (98%)
  local copies, waits for them, and re-layouts  3.86 us (1%)
    pallas_call x1, Pallas kernels, local_run(): pl.pallas_call(_kernel, out_shape=jax.ShapeDtypeStruct((ROWS, 4 * HALF),...  256 us

profile of v5, /device:TPU:0, one launch (start us, length us, event | category | flops | bytes accessed | tf_op | source)
XLA Modules:
  0.0 260.0 jit_solution(7903115668189207854)
XLA Ops:
  0.0 256.2 %backtransform.1 = f32[1536,512]{1,0:T(8,128)} custom-call(f32[6144,128]{1,0:T(8,128)} %z_in.1, f32[1536,3072]{1,0:T(8,128)} %v_in.1, f32[32,32,192]{2,1,0:T(8,128)} %bitcast.1), custom_call_target="tpu_custom_call" | custom-call | tf_op jit(solution)/shard_map/backtransform/pallas_call | solution.py:380
  256.2 3.9 %copy.5 = f32[1536,512]{1,0:T(8,128)} copy(f32[1536,512]{1,0:T(8,128)} %backtransform.1) | data formatting | bytes 6291456

commit v6 on v5

--- a/solution.py
+++ b/solution.py
@@ -15,6 +15,7 @@
 NT = ROWS // TILE
 NB = 24
 VT = 4 * sum(range(1, NT + 1))
+PITCH = 40
 AHEAD = 12
 
 
@@ -126,16 +127,6 @@
         if b == NB - 2:
             for j in range(4):
                 z_chunk(NT - 1, j, x).start()
-    for t in range(NT):
-        for rho in range(2):
-            z_own(t, rho).wait()
-    t_copy_in.wait()
-
-    def t_row(i, carry):
-        tt[pl.ds(i, NB * 8, stride=W), :] = t_raw[i].T
-        return carry
-
-    lax.fori_loop(0, W, t_row, 0)
 
     def rows(b, t, rho):
         return pl.ds(pl.multiple_of((rho * VT + _base(b) + t - b // 4) * TILE, TILE), TILE)
@@ -247,27 +238,37 @@
         same = ra == rb
 
         def diagonal(par):
-            at = [pl.multiple_of((8 * b + 2 * i + par) * W, W) for i in range(4)]
+            at = [pl.multiple_of((8 * b + 2 * i + par) * PITCH, 8) for i in range(4)]
             stack = jnp.concatenate([tt[pl.ds(row, W), :] for row in at], axis=0)
             return jnp.where(same, jnp.concatenate([stack] * 4, axis=1), 0.0).T
 
+        lo, hi = slice(0, HALF // 2), slice(HALF // 2, HALF)
         even_part, odd_part = upack[0], upack[1]
-        eo = jnp.where(ra <= rb, even_part, 0.0).T
-        u_tr = jnp.concatenate([
-            jnp.concatenate([jnp.where(ra > rb, even_part, 0.0), jnp.where(ra < rb, odd_part, 0.0).T], axis=1),
-            jnp.concatenate([eo, jnp.where(ra > rb, odd_part, 0.0)], axis=1)], axis=0)
+        ee, oo = jnp.where(ra > rb, even_part, 0.0), jnp.where(ra > rb, odd_part, 0.0)
+        oe, eo = jnp.where(ra <= rb, even_part, 0.0).T, jnp.where(ra < rb, odd_part, 0.0).T
+
+        def quad(a, b_, c_, d, rows_, cols_):
+            return jnp.concatenate([
+                jnp.concatenate([a[rows_, cols_], b_[rows_, cols_]], axis=1),
+                jnp.concatenate([c_[rows_, cols_], d[rows_, cols_]], axis=1)], axis=0)
+
         even, odd = diagonal(0), diagonal(1)
-        pairs = jnp.where(same, eo, 0.0)
-        tbuf[slot, :HALF, :HALF] = even
-        tbuf[slot, :HALF, HALF:] = jnp.zeros((HALF, HALF), jnp.float32)
-        tbuf[slot, HALF:, :HALF] = -_dot(_dot(odd, pairs, 1, 0), even, 1, 0)
-        tbuf[slot, HALF:, HALF:] = odd
-        pa = _panel(lax.broadcasted_iota(jnp.int32, (TILE, TILE), 0))
-        pb = _panel(lax.broadcasted_iota(jnp.int32, (TILE, TILE), 1))
-        for size in (2, 4):
-            level = (pa // (2 * size) == pb // (2 * size)) & (pa // size > pb // size)
-            t_now = tbuf[slot]
-            tbuf[slot] = t_now - _dot(_dot(t_now, jnp.where(level, u_tr, 0.0), 1, 0), t_now, 1, 0)
+        cross = -_dot(_dot(odd, jnp.where(same, oe, 0.0), 1, 0), even, 1, 0)
+        zero = jnp.zeros((HALF, HALF), jnp.float32)
+        pa, pb = ra % 2, rb % 2
+        t_diag = []
+        for part in (lo, hi):
+            t_now = quad(even, zero, cross, odd, part, part)
+            u_now = jnp.where(pa > pb, quad(ee, eo, oe, oo, part, part), 0.0)
+            t_diag.append(t_now - _dot(_dot(t_now, u_now, 1, 0), t_now, 1, 0))
+        t_lo, t_hi = t_diag
+        t_off = -_dot(_dot(t_hi, quad(ee, eo, oe, oo, hi, lo), 1, 0), t_lo, 1, 0)
+        half0 = jnp.zeros((HALF // 2, HALF // 2), jnp.float32)
+        for rows_, out_rows in ((lo, 0), (hi, HALF)):
+            tbuf[slot, out_rows : out_rows + HALF // 2, :] = jnp.concatenate(
+                [t_lo[rows_, lo], half0, t_lo[rows_, hi], half0], axis=1)
+            tbuf[slot, out_rows + HALF // 2 : out_rows + HALF, :] = jnp.concatenate(
+                [t_off[rows_, lo], t_hi[rows_, lo], t_off[rows_, hi], t_hi[rows_, hi]], axis=1)
         t_copy(b).start()
 
     def step(s, carry):
@@ -281,6 +282,8 @@
             def _():
                 for j in range(4):
                     z_chunk(b_sweep // 4, j, 1 - x).wait_recv()
+                for rho in range(2):
+                    z_own(b_sweep // 4, rho).wait()
                 for g in range(2):
                     zt[g, :, cols(b_sweep // 4)] = zst[g, b_sweep // 4].T
 
@@ -293,6 +296,16 @@
                 v_fwd(b, c).start()
 
             static_block(k - 2, forward)
+
+        @pl.when(k == NB)
+        def _():
+            t_copy_in.wait()
+
+            def t_row(i, carry):
+                tt[pl.ds(i, NB * 8, stride=PITCH), :] = t_raw[i].T
+                return carry
+
+            lax.fori_loop(0, W, t_row, 0)
 
         @pl.when((k >= 1) & (k <= NB) & ((k - 1) % 2 != c))
         def _():
@@ -388,7 +401,7 @@
                 pltpu.VMEM((2, HALF, 2 * ROWS), f32),
                 pltpu.VMEM((2, NT, 2 * TILE, HALF), f32),
                 pltpu.VMEM((W, W, NB * 8), f32),
-                pltpu.VMEM((NB * 8 * W, W), f32),
+                pltpu.VMEM((NB * 8 * PITCH, W), f32),
                 pltpu.VMEM((2, HALF, TILE), f32),
                 pltpu.VMEM((2, 2, HALF, TILE), f32),
                 pltpu.VMEM((HALF, TILE), f32),

time: 260 us -> 258 us (level)
  no operation moved by 1% of the time
where the time goes in v6:
time: 258 us
  Pallas kernels  254 us (98%)
  local copies, waits for them, and re-layouts  3.86 us (1%)
    pallas_call x1, Pallas kernels, local_run(): pl.pallas_call(_kernel, out_shape=jax.ShapeDtypeStruct((ROWS, 4 * HALF),...  254 us

profile of v6, /device:TPU:0, one launch (start us, length us, event | category | flops | bytes accessed | tf_op | source)
XLA Modules:
  0.0 258.2 jit_solution(7273164271483168746)
XLA Ops:
  0.0 254.3 %backtransform.1 = f32[1536,512]{1,0:T(8,128)} custom-call(f32[6144,128]{1,0:T(8,128)} %z_in.1, f32[1536,3072]{1,0:T(8,128)} %v_in.1, f32[32,32,192]{2,1,0:T(8,128)} %bitcast.1), custom_call_target="tpu_custom_call" | custom-call | tf_op jit(solution)/shard_map/backtransform/pallas_call | solution.py:393
  254.4 3.9 %copy.5 = f32[1536,512]{1,0:T(8,128)} copy(f32[1536,512]{1,0:T(8,128)} %backtransform.1) | data formatting | bytes 6291456

commit v7 on v6

--- a/solution.py
+++ b/solution.py
@@ -271,10 +271,24 @@
                 [t_off[rows_, lo], t_hi[rows_, lo], t_off[rows_, hi], t_hi[rows_, hi]], axis=1)
         t_copy(b).start()
 
+    def t_layout():
+        t_copy_in.wait()
+
+        def t_row(i, carry):
+            tt[pl.ds(i, NB * 8, stride=PITCH), :] = t_raw[i].T
+            return carry
+
+        lax.fori_loop(0, W, t_row, 0)
+
+    def z_send(n):
+        z_chunk((19 - n) // 4, n % 4, x).start()
+
     def step(s, carry):
         k = NB + 1 - s
         b_sweep = jnp.where(k == NB, NB - 1, k)
         sweeps = (k < NB - 1) | (k == NB)
+        b_in, takes_in = jnp.where(k >= 4, k - 2, k - 1), (k >= 1) & (k != 3)
+        b_merge, merges = jnp.where(k >= 3, k - 1, k), (k <= NB) & (k != 2)
 
         @pl.when(sweeps)
         def _():
@@ -289,27 +303,17 @@
 
             sweep(0, b_sweep)
 
-        @pl.when(k >= 2)
+        @pl.when(takes_in)
         def _():
             def forward(b):
                 v_y(b, 1 - y).wait_recv()
                 v_fwd(b, c).start()
 
-            static_block(k - 2, forward)
-
-        @pl.when(k == NB)
-        def _():
-            t_copy_in.wait()
-
-            def t_row(i, carry):
-                tt[pl.ds(i, NB * 8, stride=PITCH), :] = t_raw[i].T
-                return carry
-
-            lax.fori_loop(0, W, t_row, 0)
-
-        @pl.when((k >= 1) & (k <= NB) & ((k - 1) % 2 != c))
-        def _():
-            u_half(k - 1)
+            static_block(b_in, forward)
+
+        @pl.when(merges & (b_merge % 2 != c))
+        def _():
+            u_half(b_merge)
 
         @pl.when(sweeps)
         def _():
@@ -319,22 +323,33 @@
         def _():
             static_block(k - AHEAD, v_issue)
 
-        @pl.when(k >= 2)
+        @pl.when(takes_in)
         def _():
             def arrived(b):
                 v_own(b, 1 - c).wait_recv()
                 v_fwd(b, 1 - c).wait_recv()
 
-            static_block(k - 2, arrived)
-            gram(k - 2)
-
-        @pl.when(k >= 6)
-        def _():
-            z_chunk((k - 6) // 4, 3 - (k - 6) % 4, x).start()
-
-        b_merge = jnp.where(k == 0, 0, k - 1)
-
-        @pl.when((k != 1) & (k <= NB) & (b_merge % 2 == c))
+            static_block(b_in, arrived)
+            gram(b_in)
+
+        @pl.when(k >= 18)
+        def _():
+            z_send(25 - k)
+
+        @pl.when((k == 14) | (k == 15))
+        def _():
+            z_send(8 + 2 * (15 - k))
+            z_send(9 + 2 * (15 - k))
+
+        @pl.when((k <= 12) & (k >= 5))
+        def _():
+            z_send(24 - k)
+
+        @pl.when(k == NB + 1)
+        def _():
+            t_layout()
+
+        @pl.when(merges & (b_merge % 2 == c))
         def _():
             u_half(b_merge)
             merge(b_merge)

time: 258 us -> 254 us (0.984)
  Pallas kernels: 254 us -> 250 us
    pallas_call x1, Pallas kernels: 254 us -> 250 us  [local_run(): pl.pallas_call(_kernel, out_shape=jax.ShapeDtypeStruct((ROWS, 4 * HALF),...]
where the time goes in v7:
time: 254 us; the launch traced here: 253 us
  Pallas kernels  250 us (98%)
  local copies, waits for them, and re-layouts  3.86 us (2%)
    pallas_call x1, Pallas kernels, local_run(): pl.pallas_call(_kernel, out_shape=jax.ShapeDtypeStruct((ROWS, 4 * HALF),...  250 us

profile of v7, /device:TPU:0, one launch (start us, length us, event | category | flops | bytes accessed | tf_op | source)
XLA Modules:
  0.0 253.4 jit_solution(3860642843547363085)
XLA Ops:
  0.0 249.6 %backtransform.1 = f32[1536,512]{1,0:T(8,128)} custom-call(f32[6144,128]{1,0:T(8,128)} %z_in.1, f32[1536,3072]{1,0:T(8,128)} %v_in.1, f32[32,32,192]{2,1,0:T(8,128)} %bitcast.1), custom_call_target="tpu_custom_call" | custom-call | tf_op jit(solution)/shard_map/backtransform/pallas_call | solution.py:408
  249.6 3.9 %copy.5 = f32[1536,512]{1,0:T(8,128)} copy(f32[1536,512]{1,0:T(8,128)} %backtransform.1) | data formatting | bytes 6291456

commit v8 on v7

--- a/solution.py
+++ b/solution.py
@@ -32,15 +32,20 @@
     return jnp.where(idx < HALF, 2 * (idx // W), 2 * ((idx - HALF) // W) + 1)
 
 
-def _pairs(lo, n, body):
-    def two(h, carry):
-        body(lo + 2 * h)
-        body(lo + 2 * h + 1)
+def _tiles(lo, n, body):
+    def three(h, carry):
+        for u in range(3):
+            body(lo + 3 * h + u)
         return carry
 
-    lax.fori_loop(0, n // 2, two, 0)
-
-    @pl.when(n % 2 == 1)
+    lax.fori_loop(0, n // 3, three, 0)
+
+    @pl.when(n % 3 == 2)
+    def _():
+        body(lo + n - 2)
+        body(lo + n - 1)
+
+    @pl.when(n % 3 == 1)
     def _():
         body(lo + n - 1)
 
@@ -180,7 +185,7 @@
             partial_s(g, k, t - 1)
             update(g, k + 1, t)
 
-        _pairs(first + late, NT - first - late, both)
+        _tiles(first + late, NT - first - late, both)
         partial_s(g, k, NT - 1)
         s_copy(g, k).start()
 
@@ -202,7 +207,7 @@
             gacc[...] += _dot(own, v_tile(b, t), 0, 0)
 
         gacc[...] = jnp.zeros((HALF, TILE), jnp.float32)
-        _pairs(b // 4, NT - b // 4, tile)
+        _tiles(b // 4, NT - b // 4, tile)
 
         def cols_of(par):
             return gacc[:, pl.ds(pl.multiple_of(par * HALF, HALF), HALF)]
@@ -315,6 +320,11 @@
         def _():
             u_half(b_merge)
 
+        @pl.when((k == 1) & (c == 1))
+        def _():
+            u_half(1)
+            merge(1)
+
         @pl.when(sweeps)
         def _():
             sweep(1, b_sweep)
@@ -349,7 +359,7 @@
         def _():
             t_layout()
 
-        @pl.when(merges & (b_merge % 2 == c))
+        @pl.when(merges & (k != 1) & (b_merge % 2 == c))
         def _():
             u_half(b_merge)
             merge(b_merge)
@@ -381,7 +391,7 @@
             update(g, 0, t)
             zst[g, t] = zt[g, :, cols(t)].T
 
-        _pairs(0, NT, last)
+        _tiles(0, NT, last)
         for t in range(NT):
             out_local(g, t).start()
             out_sib(g, t).start()

time: 254 us -> 248 us (0.976)
  Pallas kernels: 250 us -> 244 us
    pallas_call x1, Pallas kernels: 250 us -> 244 us  [local_run(): pl.pallas_call(_kernel, out_shape=jax.ShapeDtypeStruct((ROWS, 4 * HALF),...]
where the time goes in v8:
time: 248 us
  Pallas kernels  244 us (98%)
  local copies, waits for them, and re-layouts  3.86 us (2%)
    pallas_call x1, Pallas kernels, local_run(): pl.pallas_call(_kernel, out_shape=jax.ShapeDtypeStruct((ROWS, 4 * HALF),...  244 us

profile of v8, /device:TPU:0, one launch (start us, length us, event | category | flops | bytes accessed | tf_op | source)
XLA Modules:
  0.0 248.3 jit_solution(872363875894157803)
XLA Ops:
  0.0 244.4 %backtransform.1 = f32[1536,512]{1,0:T(8,128)} custom-call(f32[6144,128]{1,0:T(8,128)} %z_in.1, f32[1536,3072]{1,0:T(8,128)} %v_in.1, f32[32,32,192]{2,1,0:T(8,128)} %bitcast.1), custom_call_target="tpu_custom_call" | custom-call | tf_op jit(solution)/shard_map/backtransform/pallas_call | solution.py:418
  244.4 3.9 %copy.5 = f32[1536,512]{1,0:T(8,128)} copy(f32[1536,512]{1,0:T(8,128)} %backtransform.1) | data formatting | bytes 6291456

commit v9 on v8

--- a/solution.py
+++ b/solution.py
@@ -13,8 +13,9 @@
 TILE = 256
 HALF = 128
 NT = ROWS // TILE
+NU = ROWS // HALF
 NB = 24
-VT = 4 * sum(range(1, NT + 1))
+VU = 2 * sum(range(1, NU + 1))
 PITCH = 40
 AHEAD = 12
 
@@ -24,30 +25,28 @@
 
 
 def _base(b):
-    q, i = b // 4, b % 4
-    return 4 * (NT * q - (q * (q - 1)) // 2) + i * (NT - q)
+    p = b // 2
+    return 2 * NU * p - p * (p - 1) + (b % 2) * (NU - p)
 
 
 def _panel(idx):
     return jnp.where(idx < HALF, 2 * (idx // W), 2 * ((idx - HALF) // W) + 1)
 
 
-def _tiles(lo, n, body):
-    def three(h, carry):
-        for u in range(3):
-            body(lo + 3 * h + u)
+def _units(lo, n, body):
+    def six(h, carry):
+        for u in range(6):
+            body(lo + 6 * h + u)
         return carry
 
-    lax.fori_loop(0, n // 3, three, 0)
-
-    @pl.when(n % 3 == 2)
-    def _():
-        body(lo + n - 2)
-        body(lo + n - 1)
-
-    @pl.when(n % 3 == 1)
-    def _():
-        body(lo + n - 1)
+    lax.fori_loop(0, n // 6, six, 0)
+    rest = n % 6
+    for size, here, start in ((4, rest >= 4, lo + n - rest), (2, (rest // 2) % 2 == 1, lo + n - rest % 4), (1, rest % 2 == 1, lo + n - 1)):
+
+        @pl.when(here)
+        def _(size=size, start=start):
+            for u in range(size):
+                body(start + u)
 
 
 def _kernel(z_in, v_in, t_in, out, vbuf, vtr, zt, zst, t_raw, tt, acc, srecv, wbuf, gacc, usend, urecv, uhalf, upack, tbuf,
@@ -68,7 +67,7 @@
         return pltpu.make_async_remote_copy(src, dst, send, recv, device_id=dev, device_id_type=MESH)
 
     def slab(b, rho, par):
-        start = (rho * VT + _base(b)) * TILE + 64 * (b % 4)
+        start = (rho * VU + _base(b)) * HALF + 64 * (b % 2)
         return vbuf.at[pl.ds(pl.multiple_of(start, 64), ROWS - 64 * b), pl.ds(pl.multiple_of(par * HALF, HALF), HALF)]
 
     def v_local(b):
@@ -99,16 +98,16 @@
                     def _(ii=ii):
                         fn(4 * qq + ii)
 
-    def z_own(t, rho):
+    def z_own(u, rho):
         return pltpu.make_async_copy(
-            z_in.at[pl.ds(pl.multiple_of((2 * x + rho) * ROWS + t * TILE, TILE), TILE), :],
-            zst.at[x, t, pl.ds(rho * TILE, TILE), :], zo_sem.at[2 * t + rho])
+            z_in.at[pl.ds(pl.multiple_of((2 * x + rho) * ROWS + u * HALF, HALF), HALF), :],
+            zst.at[x, u, pl.ds(rho * HALF, HALF), :], zo_sem.at[2 * u + rho])
 
     def z_chunk(t, j, g):
         src = (2 * (1 - x) + j // 2) * ROWS + t * TILE + (j % 2) * HALF
         return remote(
             z_in.at[pl.ds(pl.multiple_of(src, HALF), HALF), :],
-            zst.at[g, t, pl.ds(pl.multiple_of(j * HALF, HALF), HALF), :],
+            zst.at[g, 2 * t + j % 2, pl.ds(pl.multiple_of((j // 2) * HALF, HALF), HALF), :],
             zs_sem.at[4 * t + j], zr_sem.at[4 * t + j], xn)
 
     t_copy_in = pltpu.make_async_copy(t_in, t_raw, tt_sem)
@@ -116,15 +115,15 @@
     for b in range(NB - 1, NB - 5, -1):
         v_local(b).start()
     t_copy_in.start()
-    for t in range(NT - 1, -1, -1):
+    for u in range(NU - 1, -1, -1):
         for rho in range(2):
-            z_own(t, rho).start()
+            z_own(u, rho).start()
     for b in range(NB - 5, -1, -1):
         v_local(b).start()
     for b in range(NB):
-        if b % 4:
+        if b % 2:
             for rho in range(2):
-                vbuf[pl.ds((rho * VT + _base(b)) * TILE, 64 * (b % 4)), :] = jnp.zeros((64 * (b % 4), TILE), jnp.float32)
+                vbuf[pl.ds((rho * VU + _base(b)) * HALF, 64), :] = jnp.zeros((64, TILE), jnp.float32)
 
     pl.semaphore_wait(barrier, 3)
     for b in range(NB - 1, NB - 1 - AHEAD, -1):
@@ -133,14 +132,14 @@
             for j in range(4):
                 z_chunk(NT - 1, j, x).start()
 
-    def rows(b, t, rho):
-        return pl.ds(pl.multiple_of((rho * VT + _base(b) + t - b // 4) * TILE, TILE), TILE)
-
-    def v_tile(b, t):
-        return jnp.concatenate([vbuf[rows(b, t, rho), :] for rho in range(2)], axis=0)
-
-    def cols(t):
-        return pl.ds(pl.multiple_of(t * 2 * TILE, 2 * TILE), 2 * TILE)
+    def rows(b, u, rho):
+        return pl.ds(pl.multiple_of((rho * VU + _base(b) + u - b // 2) * HALF, HALF), HALF)
+
+    def v_unit(b, u):
+        return jnp.concatenate([vbuf[rows(b, u, rho), :] for rho in range(2)], axis=0)
+
+    def cols(u):
+        return pl.ds(pl.multiple_of(u * TILE, TILE), TILE)
 
     def s_copy(g, b):
         return remote(acc.at[g], srecv.at[g, b % 2], ss_sem.at[g], sr_sem.at[g, b % 2], xn)
@@ -157,16 +156,16 @@
         wbuf[...] = _dot(s_sum, tbuf[b % 4], 1, 0)
         s_copy(g, b).wait_send()
 
-    def update(g, b, t):
+    def update(g, b, u):
         if g == 0:
-            v_tr = v_tile(b, t).T
-            vtr[:, cols(t)] = v_tr
+            v_tr = v_unit(b, u).T
+            vtr[:, cols(u)] = v_tr
         else:
-            v_tr = vtr[:, cols(t)]
-        zt[g, :, cols(t)] = zt[g, :, cols(t)] - _dot(wbuf[...], v_tr, 1, 0)
-
-    def partial_s(g, b, t):
-        acc[g] += _dot(zt[g, :, cols(t)], v_tile(b, t), 1, 0)
+            v_tr = vtr[:, cols(u)]
+        zt[g, :, cols(u)] = zt[g, :, cols(u)] - _dot(wbuf[...], v_tr, 1, 0)
+
+    def partial_s(g, b, u):
+        acc[g] += _dot(zt[g, :, cols(u)], v_unit(b, u), 1, 0)
 
     def sweep(g, k):
         @pl.when(k < NB - 1)
@@ -174,19 +173,19 @@
             weights(g, k + 1)
 
         acc[g] = jnp.zeros((HALF, TILE), jnp.float32)
-        first = (k + 1) // 4
-        late = jnp.where(k % 4 == 3, 0, 1)
+        first = (k + 1) // 2
+        late = 1 - k % 2
 
         @pl.when(late == 1)
         def _():
             update(g, k + 1, first)
 
-        def both(t):
-            partial_s(g, k, t - 1)
-            update(g, k + 1, t)
-
-        _tiles(first + late, NT - first - late, both)
-        partial_s(g, k, NT - 1)
+        def both(u):
+            partial_s(g, k, u - 1)
+            update(g, k + 1, u)
+
+        _units(first + late, NU - first - late, both)
+        partial_s(g, k, NU - 1)
         s_copy(g, k).start()
 
     ra = lax.broadcasted_iota(jnp.int32, (HALF, HALF), 0) // W
@@ -201,13 +200,13 @@
         return remote(tbuf.at[b % 4], tbuf.at[b % 4], ts_sem, tr_sem.at[b % 4], sib)
 
     def gram(b):
-        def tile(t):
+        def unit(u):
             own = jnp.concatenate(
-                [vbuf[rows(b, t, rho), pl.ds(pl.multiple_of(c * HALF, HALF), HALF)] for rho in range(2)], axis=0)
-            gacc[...] += _dot(own, v_tile(b, t), 0, 0)
+                [vbuf[rows(b, u, rho), pl.ds(pl.multiple_of(c * HALF, HALF), HALF)] for rho in range(2)], axis=0)
+            gacc[...] += _dot(own, v_unit(b, u), 0, 0)
 
         gacc[...] = jnp.zeros((HALF, TILE), jnp.float32)
-        _tiles(b // 4, NT - b // 4, tile)
+        _units(b // 2, NU - b // 2, unit)
 
         def cols_of(par):
             return gacc[:, pl.ds(pl.multiple_of(par * HALF, HALF), HALF)]
@@ -301,10 +300,12 @@
             def _():
                 for j in range(4):
                     z_chunk(b_sweep // 4, j, 1 - x).wait_recv()
-                for rho in range(2):
-                    z_own(b_sweep // 4, rho).wait()
-                for g in range(2):
-                    zt[g, :, cols(b_sweep // 4)] = zst[g, b_sweep // 4].T
+                for h in range(2):
+                    u = 2 * (b_sweep // 4) + h
+                    for rho in range(2):
+                        z_own(u, rho).wait()
+                    for g in range(2):
+                        zt[g, :, cols(u)] = zst[g, u].T
 
             sweep(0, b_sweep)
 
@@ -368,33 +369,33 @@
 
     lax.fori_loop(0, NB + 2, step, 0)
 
-    def out_part(g, t, core):
-        return out.at[pl.ds(t * TILE, TILE), pl.ds(pl.multiple_of((2 * g + core) * HALF, HALF), HALF)]
-
-    def z_part(g, t, rho):
-        return zst.at[g, t, pl.ds(pl.multiple_of(rho * TILE, TILE), TILE), :]
-
-    def out_local(g, t):
-        return pltpu.make_async_copy(z_part(g, t, c), out_part(g, t, c), out_sem.at[g * NT + t])
-
-    def out_sib(g, t):
-        return remote(z_part(g, t, 1 - c), out_part(g, t, c), outs_sem.at[g * NT + t], outr_sem.at[g * NT + t], sib)
-
-    def out_from_sib(g, t):
-        part = out_part(g, t, 1 - c)
-        return remote(part, part, outs_sem.at[g * NT + t], outr_sem.at[g * NT + t], sib)
+    def out_part(g, u, core):
+        return out.at[pl.ds(u * HALF, HALF), pl.ds(pl.multiple_of((2 * g + core) * HALF, HALF), HALF)]
+
+    def z_part(g, u, rho):
+        return zst.at[g, u, pl.ds(pl.multiple_of(rho * HALF, HALF), HALF), :]
+
+    def out_local(g, u):
+        return pltpu.make_async_copy(z_part(g, u, c), out_part(g, u, c), out_sem.at[g * NU + u])
+
+    def out_sib(g, u):
+        return remote(z_part(g, u, 1 - c), out_part(g, u, c), outs_sem.at[g * NU + u], outr_sem.at[g * NU + u], sib)
+
+    def out_from_sib(g, u):
+        part = out_part(g, u, 1 - c)
+        return remote(part, part, outs_sem.at[g * NU + u], outr_sem.at[g * NU + u], sib)
 
     for g in range(2):
         weights(g, 0)
 
-        def last(t, g=g):
-            update(g, 0, t)
-            zst[g, t] = zt[g, :, cols(t)].T
-
-        _tiles(0, NT, last)
-        for t in range(NT):
-            out_local(g, t).start()
-            out_sib(g, t).start()
+        def last(u, g=g):
+            update(g, 0, u)
+            zst[g, u] = zt[g, :, cols(u)].T
+
+        _units(0, NU, last)
+        for u in range(NU):
+            out_local(g, u).start()
+            out_sib(g, u).start()
 
     half_copy.wait_send()
     t_copy(0).wait_send()
@@ -404,10 +405,10 @@
         v_fwd(b, c).wait_send()
         z_chunk(b // 4, b % 4, x).wait_send()
     for g in range(2):
-        for t in range(NT):
-            out_local(g, t).wait()
-            out_sib(g, t).wait_send()
-            out_from_sib(g, t).wait_recv()
+        for u in range(NU):
+            out_local(g, u).wait()
+            out_sib(g, u).wait_send()
+            out_from_sib(g, u).wait_recv()
 
 
 def solution(mesh):
@@ -421,10 +422,10 @@
             in_specs=[any_spec] * 3,
             out_specs=any_spec,
             scratch_shapes=[
-                pltpu.VMEM((2 * VT * TILE, TILE), f32),
+                pltpu.VMEM((2 * VU * HALF, TILE), f32),
                 pltpu.VMEM((TILE, 2 * ROWS), f32),
                 pltpu.VMEM((2, HALF, 2 * ROWS), f32),
-                pltpu.VMEM((2, NT, 2 * TILE, HALF), f32),
+                pltpu.VMEM((2, NU, TILE, HALF), f32),
                 pltpu.VMEM((W, W, NB * 8), f32),
                 pltpu.VMEM((NB * 8 * PITCH, W), f32),
                 pltpu.VMEM((2, HALF, TILE), f32),
@@ -437,7 +438,7 @@
                 pltpu.VMEM((2, HALF, HALF), f32),
                 pltpu.VMEM((4, TILE, TILE), f32),
                 *[dma((NB,))] * 9,
-                dma((2,)), dma((2, 2)), dma((2,)), dma((4,)), dma, dma, dma, dma((4,)), dma, *[dma((2 * NT,))] * 4,
+                dma((2,)), dma((2, 2)), dma((2,)), dma((4,)), dma, dma, dma, dma((4,)), dma, *[dma((2 * NU,))] * 4,
             ],
             compiler_params=pltpu.CompilerParams(collective_id=0, has_side_effects=True, vmem_limit_bytes=63 * 2**20),
             name="backtransform",

time: 248 us -> 249 us (level)
  no operation moved by 1% of the time
where the time goes in v9:
time: 249 us
  Pallas kernels  245 us (98%)
  local copies, waits for them, and re-layouts  3.86 us (2%)
    pallas_call x1, Pallas kernels, local_run(): pl.pallas_call(_kernel, out_shape=jax.ShapeDtypeStruct((ROWS, 4 * HALF),...  245 us

profile of v9, /device:TPU:0, one launch (start us, length us, event | category | flops | bytes accessed | tf_op | source)
XLA Modules:
  0.0 249.4 jit_solution(613151132556098290)
XLA Ops:
  0.0 245.5 %backtransform.1 = f32[1536,512]{1,0:T(8,128)} custom-call(f32[6144,128]{1,0:T(8,128)} %z_in.1, f32[1536,3072]{1,0:T(8,128)} %v_in.1, f32[32,32,192]{2,1,0:T(8,128)} %bitcast.1), custom_call_target="tpu_custom_call" | custom-call | tf_op jit(solution)/shard_map/backtransform/pallas_call | solution.py:419
  245.5 3.9 %copy.5 = f32[1536,512]{1,0:T(8,128)} copy(f32[1536,512]{1,0:T(8,128)} %backtransform.1) | data formatting | bytes 6291456

commit v10 on v9

--- a/solution.py
+++ b/solution.py
@@ -33,20 +33,22 @@
     return jnp.where(idx < HALF, 2 * (idx // W), 2 * ((idx - HALF) // W) + 1)
 
 
-def _units(lo, n, body):
+def _units(lo, n, body, end=None):
     def six(h, carry):
         for u in range(6):
             body(lo + 6 * h + u)
         return carry
 
     lax.fori_loop(0, n // 6, six, 0)
-    rest = n % 6
-    for size, here, start in ((4, rest >= 4, lo + n - rest), (2, (rest // 2) % 2 == 1, lo + n - rest % 4), (1, rest % 2 == 1, lo + n - 1)):
-
-        @pl.when(here)
-        def _(size=size, start=start):
-            for u in range(size):
-                body(start + u)
+    for rest in range(6):
+        if rest or end:
+
+            @pl.when(n % 6 == rest)
+            def _(rest=rest):
+                for u in range(rest):
+                    body(lo + n - rest + u)
+                if end:
+                    end()
 
 
 def _kernel(z_in, v_in, t_in, out, vbuf, vtr, zt, zst, t_raw, tt, acc, srecv, wbuf, gacc, usend, urecv, uhalf, upack, tbuf,
@@ -184,8 +186,7 @@
             partial_s(g, k, u - 1)
             update(g, k + 1, u)
 
-        _units(first + late, NU - first - late, both)
-        partial_s(g, k, NU - 1)
+        _units(first + late, NU - first - late, both, lambda: partial_s(g, k, NU - 1))
         s_copy(g, k).start()
 
     ra = lax.broadcasted_iota(jnp.int32, (HALF, HALF), 0) // W

time: 249 us -> 249 us (level)
  no operation moved by 1% of the time
where the time goes in v10:
time: 249 us
  Pallas kernels  245 us (98%)
  local copies, waits for them, and re-layouts  3.86 us (2%)
    pallas_call x1, Pallas kernels, local_run(): pl.pallas_call(_kernel, out_shape=jax.ShapeDtypeStruct((ROWS, 4 * HALF),...  245 us

profile of v10, /device:TPU:0, one launch (start us, length us, event | category | flops | bytes accessed | tf_op | source)
XLA Modules:
  0.0 248.9 jit_solution(8433329033754995974)
XLA Ops:
  0.0 245.0 %backtransform.1 = f32[1536,512]{1,0:T(8,128)} custom-call(f32[6144,128]{1,0:T(8,128)} %z_in.1, f32[1536,3072]{1,0:T(8,128)} %v_in.1, f32[32,32,192]{2,1,0:T(8,128)} %bitcast.1), custom_call_target="tpu_custom_call" | custom-call | tf_op jit(solution)/shard_map/backtransform/pallas_call | solution.py:420
  245.0 3.9 %copy.5 = f32[1536,512]{1,0:T(8,128)} copy(f32[1536,512]{1,0:T(8,128)} %backtransform.1) | data formatting | bytes 6291456

commit v11 on v10

--- a/solution.py
+++ b/solution.py
@@ -288,11 +288,19 @@
     def z_send(n):
         z_chunk((19 - n) // 4, n % 4, x).start()
 
+    def forward(b):
+        v_y(b, 1 - y).wait_recv()
+        v_fwd(b, c).start()
+
+    def arrived(b):
+        v_own(b, 1 - c).wait_recv()
+        v_fwd(b, 1 - c).wait_recv()
+
     def step(s, carry):
         k = NB + 1 - s
         b_sweep = jnp.where(k == NB, NB - 1, k)
         sweeps = (k < NB - 1) | (k == NB)
-        b_in, takes_in = jnp.where(k >= 4, k - 2, k - 1), (k >= 1) & (k != 3)
+        b_in, takes_in = jnp.where(k >= 4, k - 2, k - 1), (k >= 2) & (k != 3)
         b_merge, merges = jnp.where(k >= 3, k - 1, k), (k <= NB) & (k != 2)
 
         @pl.when(sweeps)
@@ -312,10 +320,6 @@
 
         @pl.when(takes_in)
         def _():
-            def forward(b):
-                v_y(b, 1 - y).wait_recv()
-                v_fwd(b, c).start()
-
             static_block(b_in, forward)
 
         @pl.when(merges & (b_merge % 2 != c))
@@ -337,10 +341,6 @@
 
         @pl.when(takes_in)
         def _():
-            def arrived(b):
-                v_own(b, 1 - c).wait_recv()
-                v_fwd(b, 1 - c).wait_recv()
-
             static_block(b_in, arrived)
             gram(b_in)
 
@@ -368,7 +368,23 @@
 
         return carry
 
-    lax.fori_loop(0, NB + 2, step, 0)
+    lax.fori_loop(0, NB + 1, step, 0)
+
+    for g in range(2):
+        weights(g, 1)
+        _units(0, NU, lambda u, g=g: update(g, 1, u))
+    forward(0)
+    arrived(0)
+    gram(0)
+    for g in range(2):
+        acc[g] = jnp.zeros((HALF, TILE), jnp.float32)
+        _units(0, NU, lambda u, g=g: partial_s(g, 0, u))
+        s_copy(g, 0).start()
+    u_half(0)
+
+    @pl.when(c == 0)
+    def _():
+        merge(0)
 
     def out_part(g, u, core):
         return out.at[pl.ds(u * HALF, HALF), pl.ds(pl.multiple_of((2 * g + core) * HALF, HALF), HALF)]

time: 249 us -> 251 us (level)
  no operation moved by 1% of the time
where the time goes in v11:
time: 251 us
  Pallas kernels  247 us (98%)
  local copies, waits for them, and re-layouts  3.86 us (2%)
    pallas_call x1, Pallas kernels, local_run(): pl.pallas_call(_kernel, out_shape=jax.ShapeDtypeStruct((ROWS, 4 * HALF),...  247 us

profile of v11, /device:TPU:0, one launch (start us, length us, event | category | flops | bytes accessed | tf_op | source)
XLA Modules:
  0.0 251.0 jit_solution(7720700422554933836)
XLA Ops:
  0.0 247.1 %backtransform.1 = f32[1536,512]{1,0:T(8,128)} custom-call(f32[6144,128]{1,0:T(8,128)} %z_in.1, f32[1536,3072]{1,0:T(8,128)} %v_in.1, f32[32,32,192]{2,1,0:T(8,128)} %bitcast.1), custom_call_target="tpu_custom_call" | custom-call | tf_op jit(solution)/shard_map/backtransform/pallas_call | solution.py:436
  247.1 3.9 %copy.5 = f32[1536,512]{1,0:T(8,128)} copy(f32[1536,512]{1,0:T(8,128)} %backtransform.1) | data formatting | bytes 6291456

commit v12 on v11

--- a/solution.py
+++ b/solution.py
@@ -348,14 +348,9 @@
         def _():
             z_send(25 - k)
 
-        @pl.when((k == 14) | (k == 15))
-        def _():
-            z_send(8 + 2 * (15 - k))
-            z_send(9 + 2 * (15 - k))
-
-        @pl.when((k <= 12) & (k >= 5))
-        def _():
-            z_send(24 - k)
+        @pl.when((k <= 15) & (k >= 4))
+        def _():
+            z_send(23 - k)
 
         @pl.when(k == NB + 1)
         def _():
@@ -370,20 +365,31 @@
 
     lax.fori_loop(0, NB + 1, step, 0)
 
-    for g in range(2):
+    def update_1(g):
         weights(g, 1)
-        _units(0, NU, lambda u, g=g: update(g, 1, u))
+        _units(0, NU, lambda u: update(g, 1, u))
+
+    def s_0(g):
+        acc[g] = jnp.zeros((HALF, TILE), jnp.float32)
+        _units(0, NU, lambda u: partial_s(g, 0, u))
+        s_copy(g, 0).start()
+
     forward(0)
+    update_1(0)
     arrived(0)
     gram(0)
-    for g in range(2):
-        acc[g] = jnp.zeros((HALF, TILE), jnp.float32)
-        _units(0, NU, lambda u, g=g: partial_s(g, 0, u))
-        s_copy(g, 0).start()
-    u_half(0)
+    update_1(1)
+    s_0(0)
+
+    @pl.when(c == 1)
+    def _():
+        u_half(0)
+
+    s_0(1)
 
     @pl.when(c == 0)
     def _():
+        u_half(0)
         merge(0)
 
     def out_part(g, u, core):

time: 251 us -> 260 us (1.036)
  Pallas kernels: 247 us -> 256 us
    pallas_call x1, Pallas kernels: 247 us -> 256 us  [local_run(): pl.pallas_call(_kernel, out_shape=jax.ShapeDtypeStruct((ROWS, 4 * HALF),...]
where the time goes in v12:
time: 260 us
  Pallas kernels  256 us (98%)
  local copies, waits for them, and re-layouts  3.86 us (1%)
    pallas_call x1, Pallas kernels, local_run(): pl.pallas_call(_kernel, out_shape=jax.ShapeDtypeStruct((ROWS, 4 * HALF),...  256 us

profile of v12, /device:TPU:0, one launch (start us, length us, event | category | flops | bytes accessed | tf_op | source)
XLA Modules:
  0.0 260.0 jit_solution(2468591103692079863)
XLA Ops:
  0.0 256.1 %backtransform.1 = f32[1536,512]{1,0:T(8,128)} custom-call(f32[6144,128]{1,0:T(8,128)} %z_in.1, f32[1536,3072]{1,0:T(8,128)} %v_in.1, f32[32,32,192]{2,1,0:T(8,128)} %bitcast.1), custom_call_target="tpu_custom_call" | custom-call | tf_op jit(solution)/shard_map/backtransform/pallas_call | solution.py:442
  256.1 3.9 %copy.5 = f32[1536,512]{1,0:T(8,128)} copy(f32[1536,512]{1,0:T(8,128)} %backtransform.1) | data formatting | bytes 6291456

commit v13 on v12

--- a/solution.py
+++ b/solution.py
@@ -326,11 +326,6 @@
         def _():
             u_half(b_merge)
 
-        @pl.when((k == 1) & (c == 1))
-        def _():
-            u_half(1)
-            merge(1)
-
         @pl.when(sweeps)
         def _():
             sweep(1, b_sweep)
@@ -348,15 +343,15 @@
         def _():
             z_send(25 - k)
 
-        @pl.when((k <= 15) & (k >= 4))
-        def _():
-            z_send(23 - k)
+        @pl.when((k <= 16) & (k >= 5))
+        def _():
+            z_send(24 - k)
 
         @pl.when(k == NB + 1)
         def _():
             t_layout()
 
-        @pl.when(merges & (k != 1) & (b_merge % 2 == c))
+        @pl.when(merges & (b_merge % 2 == c))
         def _():
             u_half(b_merge)
             merge(b_merge)
@@ -374,23 +369,30 @@
         _units(0, NU, lambda u: partial_s(g, 0, u))
         s_copy(g, 0).start()
 
+    def gram_0(core):
+        @pl.when(c == core)
+        def _():
+            arrived(0)
+            gram(0)
+
     forward(0)
+    gram_0(1)
     update_1(0)
-    arrived(0)
-    gram(0)
+    gram_0(0)
     update_1(1)
-    s_0(0)
 
     @pl.when(c == 1)
     def _():
         u_half(0)
 
-    s_0(1)
+    s_0(0)
 
     @pl.when(c == 0)
     def _():
         u_half(0)
         merge(0)
+
+    s_0(1)
 
     def out_part(g, u, core):
         return out.at[pl.ds(u * HALF, HALF), pl.ds(pl.multiple_of((2 * g + core) * HALF, HALF), HALF)]

time: 260 us -> 248 us (0.954)
  Pallas kernels: 256 us -> 244 us
    pallas_call x1, Pallas kernels: 256 us -> 244 us  [local_run(): pl.pallas_call(_kernel, out_shape=jax.ShapeDtypeStruct((ROWS, 4 * HALF),...]
where the time goes in v13:
time: 248 us
  Pallas kernels  244 us (98%)
  local copies, waits for them, and re-layouts  3.86 us (2%)
    pallas_call x1, Pallas kernels, local_run(): pl.pallas_call(_kernel, out_shape=jax.ShapeDtypeStruct((ROWS, 4 * HALF),...  244 us

profile of v13, /device:TPU:0, one launch (start us, length us, event | category | flops | bytes accessed | tf_op | source)
XLA Modules:
  0.0 247.6 jit_solution(4818399104850143203)
XLA Ops:
  0.0 243.7 %backtransform.1 = f32[1536,512]{1,0:T(8,128)} custom-call(f32[6144,128]{1,0:T(8,128)} %z_in.1, f32[1536,3072]{1,0:T(8,128)} %v_in.1, f32[32,32,192]{2,1,0:T(8,128)} %bitcast.1), custom_call_target="tpu_custom_call" | custom-call | tf_op jit(solution)/shard_map/backtransform/pallas_call | solution.py:444
  243.7 3.9 %copy.5 = f32[1536,512]{1,0:T(8,128)} copy(f32[1536,512]{1,0:T(8,128)} %backtransform.1) | data formatting | bytes 6291456

commit v14 on v13

--- a/solution.py
+++ b/solution.py
@@ -89,16 +89,12 @@
         v_y(b, y).start()
         v_own(b, c).start()
 
-    def static_block(b, fn):
-        for qq in range(NT):
-
-            @pl.when(b // 4 == qq)
-            def _(qq=qq):
-                for ii in range(4):
-
-                    @pl.when(b % 4 == ii)
-                    def _(ii=ii):
-                        fn(4 * qq + ii)
+    def static_block(b, fn, low=0, high=NB):
+        if high - low == 1:
+            fn(low)
+            return
+        mid = (low + high) // 2
+        lax.cond(b < mid, lambda: static_block(b, fn, low, mid), lambda: static_block(b, fn, mid, high))
 
     def z_own(u, rho):
         return pltpu.make_async_copy(

time: 248 us -> 248 us (level)
  no operation moved by 1% of the time
where the time goes in v14:
time: 248 us
  Pallas kernels  244 us (98%)
  local copies, waits for them, and re-layouts  3.86 us (2%)
    pallas_call x1, Pallas kernels, local_run(): pl.pallas_call(_kernel, out_shape=jax.ShapeDtypeStruct((ROWS, 4 * HALF),...  244 us

profile of v14, /device:TPU:0, one launch (start us, length us, event | category | flops | bytes accessed | tf_op | source)
XLA Modules:
  0.0 247.6 jit_solution(3974922514733092529)
XLA Ops:
  0.0 243.7 %backtransform.1 = f32[1536,512]{1,0:T(8,128)} custom-call(f32[6144,128]{1,0:T(8,128)} %z_in.1, f32[1536,3072]{1,0:T(8,128)} %v_in.1, f32[32,32,192]{2,1,0:T(8,128)} %bitcast.1), custom_call_target="tpu_custom_call" | custom-call | tf_op jit(solution)/shard_map/backtransform/pallas_call | solution.py:440
  243.7 3.9 %copy.5 = f32[1536,512]{1,0:T(8,128)} copy(f32[1536,512]{1,0:T(8,128)} %backtransform.1) | data formatting | bytes 6291456

commit v15 on v14

--- a/solution.py
+++ b/solution.py
@@ -375,20 +375,19 @@
     gram_0(1)
     update_1(0)
     gram_0(0)
-    update_1(1)
+    s_0(0)
 
     @pl.when(c == 1)
     def _():
         u_half(0)
 
-    s_0(0)
+    update_1(1)
+    s_0(1)
 
     @pl.when(c == 0)
     def _():
         u_half(0)
         merge(0)
-
-    s_0(1)
 
     def out_part(g, u, core):
         return out.at[pl.ds(u * HALF, HALF), pl.ds(pl.multiple_of((2 * g + core) * HALF, HALF), HALF)]

time: 248 us -> 247 us (level)
  no operation moved by 1% of the time
where the time goes in v15:
time: 247 us
  Pallas kernels  243 us (98%)
  local copies, waits for them, and re-layouts  3.86 us (2%)
    pallas_call x1, Pallas kernels, local_run(): pl.pallas_call(_kernel, out_shape=jax.ShapeDtypeStruct((ROWS, 4 * HALF),...  243 us

profile of v15, /device:TPU:0, one launch (start us, length us, event | category | flops | bytes accessed | tf_op | source)
XLA Modules:
  0.0 246.9 jit_solution(15122717922992192105)
XLA Ops:
  0.0 243.0 %backtransform.1 = f32[1536,512]{1,0:T(8,128)} custom-call(f32[6144,128]{1,0:T(8,128)} %z_in.1, f32[1536,3072]{1,0:T(8,128)} %v_in.1, f32[32,32,192]{2,1,0:T(8,128)} %bitcast.1), custom_call_target="tpu_custom_call" | custom-call | tf_op jit(solution)/shard_map/backtransform/pallas_call | solution.py:439
  243.0 3.9 %copy.5 = f32[1536,512]{1,0:T(8,128)} copy(f32[1536,512]{1,0:T(8,128)} %backtransform.1) | data formatting | bytes 6291456

commit v16 on v15

--- a/solution.py
+++ b/solution.py
@@ -326,6 +326,10 @@
         def _():
             sweep(1, b_sweep)
 
+        @pl.when(k == 1)
+        def _():
+            forward(0)
+
         @pl.when((k >= AHEAD) & (k < NB))
         def _():
             static_block(k - AHEAD, v_issue)
@@ -371,17 +375,16 @@
             arrived(0)
             gram(0)
 
-    forward(0)
+    gram_0(0)
+    update_1(0)
     gram_0(1)
-    update_1(0)
-    gram_0(0)
     s_0(0)
+    update_1(1)
 
     @pl.when(c == 1)
     def _():
         u_half(0)
 
-    update_1(1)
     s_0(1)
 
     @pl.when(c == 0)

time: 247 us -> 246 us (level)
  no operation moved by 1% of the time
where the time goes in v16:
time: 246 us
  Pallas kernels  242 us (98%)
  local copies, waits for them, and re-layouts  3.86 us (2%)
    pallas_call x1, Pallas kernels, local_run(): pl.pallas_call(_kernel, out_shape=jax.ShapeDtypeStruct((ROWS, 4 * HALF),...  242 us

profile of v16, /device:TPU:0, one launch (start us, length us, event | category | flops | bytes accessed | tf_op | source)
XLA Modules:
  0.0 246.0 jit_solution(716300208937715654)
XLA Ops:
  0.0 242.1 %backtransform.1 = f32[1536,512]{1,0:T(8,128)} custom-call(f32[6144,128]{1,0:T(8,128)} %z_in.1, f32[1536,3072]{1,0:T(8,128)} %v_in.1, f32[32,32,192]{2,1,0:T(8,128)} %bitcast.1), custom_call_target="tpu_custom_call" | custom-call | tf_op jit(solution)/shard_map/backtransform/pallas_call | solution.py:442
  242.1 3.9 %copy.5 = f32[1536,512]{1,0:T(8,128)} copy(f32[1536,512]{1,0:T(8,128)} %backtransform.1) | data formatting | bytes 6291456

commit v17 on v16

--- a/solution.py
+++ b/solution.py
@@ -393,7 +393,7 @@
         merge(0)
 
     def out_part(g, u, core):
-        return out.at[pl.ds(u * HALF, HALF), pl.ds(pl.multiple_of((2 * g + core) * HALF, HALF), HALF)]
+        return out.at[pl.ds(u * HALF if isinstance(u, int) else pl.multiple_of(u * HALF, HALF), HALF), pl.ds(pl.multiple_of((2 * g + core) * HALF, HALF), HALF)]
 
     def z_part(g, u, rho):
         return zst.at[g, u, pl.ds(pl.multiple_of(rho * HALF, HALF), HALF), :]
@@ -415,10 +415,15 @@
             update(g, 0, u)
             zst[g, u] = zt[g, :, cols(u)].T
 
-        _units(0, NU, last)
-        for u in range(NU):
-            out_local(g, u).start()
-            out_sib(g, u).start()
+        def last_half(h, carry, g=g):
+            for u in range(NU // 2):
+                last(h * (NU // 2) + u)
+            for u in range(NU // 2):
+                out_local(g, h * (NU // 2) + u).start()
+                out_sib(g, h * (NU // 2) + u).start()
+            return carry
+
+        lax.fori_loop(0, 2, last_half, 0)
 
     half_copy.wait_send()
     t_copy(0).wait_send()

time: 246 us -> 246 us (level)
  no operation moved by 1% of the time
where the time goes in v17:
time: 246 us; the launch traced here: 245 us
  Pallas kernels  242 us (98%)
  local copies, waits for them, and re-layouts  3.86 us (2%)
    pallas_call x1, Pallas kernels, local_run(): pl.pallas_call(_kernel, out_shape=jax.ShapeDtypeStruct((ROWS, 4 * HALF),...  242 us

profile of v17, /device:TPU:0, one launch (start us, length us, event | category | flops | bytes accessed | tf_op | source)
XLA Modules:
  0.0 245.5 jit_solution(15530372332283217570)
XLA Ops:
  0.0 241.6 %backtransform.1 = f32[1536,512]{1,0:T(8,128)} custom-call(f32[6144,128]{1,0:T(8,128)} %z_in.1, f32[1536,3072]{1,0:T(8,128)} %v_in.1, f32[32,32,192]{2,1,0:T(8,128)} %bitcast.1), custom_call_target="tpu_custom_call" | custom-call | tf_op jit(solution)/shard_map/backtransform/pallas_call | solution.py:447
  241.6 3.9 %copy.5 = f32[1536,512]{1,0:T(8,128)} copy(f32[1536,512]{1,0:T(8,128)} %backtransform.1) | data formatting | bytes 6291456
